TPU v7x, 32 devices: a 4x2x2 block of a 4x4x8 slice. The times are simulated.
32 devices in a mesh: dp: 4 (over y, z), cp: 8 (over x, core).
Axes of the slice: x: 4, y: 2, z: 2, core: 2. Of those that a mesh axis runs over, the one named last changes fastest.
The devices are a block of a 4x4x8 slice.
Arguments:
- queries: bfloat16 [4, 2048, 32, 128], P('dp', 'cp'), parts along dimension 0
- keys: bfloat16 [4, 2048, 16, 128], P('dp', 'cp'), parts along dimension 0
- values: bfloat16 [4, 2048, 16, 128], P('dp', 'cp'), parts along dimension 0
- out_grad: bfloat16 [4, 2048, 32, 128], P('dp', 'cp'), parts along dimension 0
Outputs:
- output 1: bfloat16 [4, 2048, 32, 128], P('dp', 'cp'), parts along dimension 0
- output 2: float32 [4, 32, 2048], P('dp', None, 'cp'), parts along dimension 0
- output 3: bfloat16 [4, 2048, 32, 128], P('dp', 'cp'), parts along dimension 0
- output 4: bfloat16 [4, 2048, 16, 128], P('dp', 'cp'), parts along dimension 0
- output 5: bfloat16 [4, 2048, 16, 128], P('dp', 'cp'), parts along dimension 0
There are 4 independent parts. A program takes and returns all parts, laid end to end along the dimension named above; each array names one.
All inputs are finite; a program needn't handle non-finite values.
Results may differ from a plain program's by a relative error of at most 0.0193272.
Values are sent between devices in bfloat16 or wider.
A program may use at most 768 MiB of HBM per device.

v0:
```python
import jax
import jax.numpy as jnp
from jax import lax
from jax.sharding import PartitionSpec as P


def block_scores(query5, key_blk, scale, causal):
    scores = jnp.einsum("bqgrd,bkgd->bgrqk", query5, key_blk, preferred_element_type=jnp.float32) * scale
    if causal:
        tokens = query5.shape[1]
        row_idx = lax.broadcasted_iota(jnp.int32, (tokens, tokens), 0)
        col_idx = lax.broadcasted_iota(jnp.int32, (tokens, tokens), 1)
        scores = jnp.where(row_idx >= col_idx, scores, -jnp.inf)
    return scores


def forward_step(query5, key_blk, value_blk, state, scale, causal):
    run_max, run_sum, run_acc = state
    scores = block_scores(query5, key_blk, scale, causal)
    new_max = jnp.maximum(run_max, jnp.max(scores, axis=-1))
    alpha = jnp.exp(run_max - new_max)
    weights = jnp.exp(scores - new_max[..., None])
    new_sum = run_sum * alpha + jnp.sum(weights, axis=-1)
    new_acc = run_acc * alpha[..., None] + jnp.einsum("bgrqk,bkgd->bgrqd", weights.astype(jnp.bfloat16), value_blk, preferred_element_type=jnp.float32)
    return new_max, new_sum, new_acc


def backward_step(query5, grad5, row_lse, delta, key_blk, value_blk, scale, causal):
    scores = block_scores(query5, key_blk, scale, causal)
    prob_mat = jnp.exp(scores - row_lse[..., None])
    grad_prob = jnp.einsum("bqgrd,bkgd->bgrqk", grad5, value_blk, preferred_element_type=jnp.float32)
    grad_score = (prob_mat * (grad_prob - delta[..., None])).astype(jnp.bfloat16)
    prob_low = prob_mat.astype(jnp.bfloat16)
    dq_part = jnp.einsum("bgrqk,bkgd->bqgrd", grad_score, key_blk, preferred_element_type=jnp.float32) * scale
    dk_part = jnp.einsum("bgrqk,bqgrd->bkgd", grad_score, query5, preferred_element_type=jnp.float32) * scale
    dv_part = jnp.einsum("bgrqk,bqgrd->bkgd", prob_low, grad5, preferred_element_type=jnp.float32)
    return dq_part, dk_part, dv_part


def solution(mesh):
    cp_size = mesh.shape["cp"]
    shift_pairs = [(source, (source + 1) % cp_size) for source in range(cp_size)]

    def attention_shard(queries, keys, values, out_grad):
        batch, tokens, heads, head_dim = queries.shape
        kv_heads = keys.shape[2]
        ratio = heads // kv_heads
        scale = head_dim ** -0.5
        cp_rank = lax.axis_index("cp")
        query5 = queries.reshape(batch, tokens, kv_heads, ratio, head_dim)
        grad5 = out_grad.reshape(batch, tokens, kv_heads, ratio, head_dim)
        stat_shape = (batch, kv_heads, ratio, tokens)
        init_state = (jnp.full(stat_shape, -jnp.inf, jnp.float32), jnp.zeros(stat_shape, jnp.float32), jnp.zeros(stat_shape + (head_dim,), jnp.float32))
        diag_state = forward_step(query5, keys, values, init_state, scale, True)

        def forward_body(step, carry):
            key_cur, value_cur, state = carry
            key_cur = lax.ppermute(key_cur, "cp", shift_pairs)
            value_cur = lax.ppermute(value_cur, "cp", shift_pairs)
            state = lax.cond(step <= cp_rank, lambda prev: forward_step(query5, key_cur, value_cur, prev, scale, False), lambda prev: prev, state)
            return key_cur, value_cur, state

        run_max, run_sum, run_acc = lax.fori_loop(1, cp_size, forward_body, (keys, values, diag_state))[2]
        out5 = (run_acc / run_sum[..., None]).astype(jnp.bfloat16)
        attn_out = jnp.transpose(out5, (0, 3, 1, 2, 4)).reshape(batch, tokens, heads, head_dim)
        row_lse = run_max + jnp.log(run_sum)
        delta = jnp.einsum("bqgrd,bgrqd->bgrq", grad5, out5, preferred_element_type=jnp.float32)

        dq_diag, dk_diag, dv_diag = backward_step(query5, grad5, row_lse, delta, keys, values, scale, True)

        def backward_body(step, carry):
            key_cur, value_cur, dk_cur, dv_cur, dq_acc = carry
            key_cur = lax.ppermute(key_cur, "cp", shift_pairs)
            value_cur = lax.ppermute(value_cur, "cp", shift_pairs)
            dk_cur = lax.ppermute(dk_cur, "cp", shift_pairs)
            dv_cur = lax.ppermute(dv_cur, "cp", shift_pairs)

            def visit(acc_in):
                dk_in, dv_in, dq_in = acc_in
                dq_part, dk_part, dv_part = backward_step(query5, grad5, row_lse, delta, key_cur, value_cur, scale, False)
                return dk_in + dk_part, dv_in + dv_part, dq_in + dq_part

            dk_cur, dv_cur, dq_acc = lax.cond(step <= cp_rank, visit, lambda acc_in: acc_in, (dk_cur, dv_cur, dq_acc))
            return key_cur, value_cur, dk_cur, dv_cur, dq_acc

        carry_out = lax.fori_loop(1, cp_size, backward_body, (keys, values, dk_diag, dv_diag, dq_diag))
        dk_home = lax.ppermute(carry_out[2], "cp", shift_pairs)
        dv_home = lax.ppermute(carry_out[3], "cp", shift_pairs)
        grad_query = carry_out[4].reshape(batch, tokens, heads, head_dim).astype(jnp.bfloat16)
        return attn_out, row_lse.reshape(batch, heads, tokens), grad_query, dk_home.astype(jnp.bfloat16), dv_home.astype(jnp.bfloat16)

    seq_spec = P("dp", "cp")
    return jax.shard_map(attention_shard, mesh=mesh, in_specs=(seq_spec, seq_spec, seq_spec, seq_spec), out_specs=(seq_spec, P("dp", None, "cp"), seq_spec, seq_spec, seq_spec), check_vma=False)
```

profile of v0, /device:TPU:94, one launch (start us, length us, event | category | flops | bytes accessed | tf_op | source)
XLA Modules:
  0.0 1017.3 jit_solution(11844849217691965208)
XLA Ops:
  11.5 7.4 add_bitcast_fusion
  18.9 263.1 %while.42 = (s32[]{:T(128)}, bf16[1,256,16,128]{3,1,2,0:T(8,128)(2,1)}, bf16[1,256,16,128]{3,1,2,0:T(8,128)(2,1)}, f32[1,16,2,256]{3,2,1,0:T(2,128)S(1)}, f32[1,...) while((s32[]{:T(128)}, ...), condition=%wide.region_7.8_spmd, body=%wide.region_2.7_spmd.sunk | while | flops 1092640768 | bytes 84410712 | solution.py:63
  19.1 14.0 %collective-permute-done = bf16[1,256,16,128]{3,1,2,0:T(8,128)(2,1)} collective-permute-done((bf16[1,256,16,128]{3,1,2,0:T(8,128)(2,1)}, bf16[1,256,16,128]{3,1,2,0:T(8,128)(2,1)}, u32[]{:S(2)}, u32[]{:S(2)}) %collective-permute-start) | collective-permute-done | bytes 1048608 | tf_op jit(solution)/shard_map/while/body/eval_jaxpr/ppermute | solution.py:58
  33.2 11.2 %collective-permute-done.1 = bf16[1,256,16,128]{3,1,2,0:T(8,128)(2,1)S(1)} collective-permute-done((bf16[1,256,16,128]{3,1,2,0:T(8,128)(2,1)}, bf16[1,256,16,128]{3,1,2,0:T(8,128)(2,1)S(1)}, u32[]{:S(2)}, u32[]{:S(2)}) %collective-permute-start.1) | collective-permute-done | bytes 1048608 | tf_op jit(solution)/shard_map/while/body/eval_jaxpr/ppermute | solution.py:59
  44.4 10.3 %conditional.4 = ((f32[1,16,2,256]{3,2,1,0:T(2,128)S(1)}, f32[1,16,2,256]{3,2,1,0:T(2,128)S(1)}, f32[1,16,2,256,128]{4,3,2,1,0:T(8,128)})) conditional(s32[]{:T(128)} %convert_element_type.100, (f32[1,16,2,256]{3,2,1,0:T(2,128)S(1)}, f32[1,16,2,256]{3,2,1,0:T(2,128)S(1)}, f32[1,16,2,256,128]{4,3,2,1,0:T(8,128)}) %tuple.78, ...), branch_computations={%region_3.3_spmd, %region_4.6_spmd} | conditional | flops 1092640768 | bytes 71827544 | solution.py:60
  58.0 14.2 %collective-permute-done = bf16[1,256,16,128]{3,1,2,0:T(8,128)(2,1)} collective-permute-done((bf16[1,256,16,128]{3,1,2,0:T(8,128)(2,1)}, bf16[1,256,16,128]{3,1,2,0:T(8,128)(2,1)}, u32[]{:S(2)}, u32[]{:S(2)}) %collective-permute-start) | collective-permute-done | bytes 1048608 | tf_op jit(solution)/shard_map/while/body/eval_jaxpr/ppermute | solution.py:58
  72.2 11.2 %collective-permute-done.1 = bf16[1,256,16,128]{3,1,2,0:T(8,128)(2,1)S(1)} collective-permute-done((bf16[1,256,16,128]{3,1,2,0:T(8,128)(2,1)}, bf16[1,256,16,128]{3,1,2,0:T(8,128)(2,1)S(1)}, u32[]{:S(2)}, u32[]{:S(2)}) %collective-permute-start.1) | collective-permute-done | bytes 1048608 | tf_op jit(solution)/shard_map/while/body/eval_jaxpr/ppermute | solution.py:59
  83.5 10.3 %conditional.4 = ((f32[1,16,2,256]{3,2,1,0:T(2,128)S(1)}, f32[1,16,2,256]{3,2,1,0:T(2,128)S(1)}, f32[1,16,2,256,128]{4,3,2,1,0:T(8,128)})) conditional(s32[]{:T(128)} %convert_element_type.100, (f32[1,16,2,256]{3,2,1,0:T(2,128)S(1)}, f32[1,16,2,256]{3,2,1,0:T(2,128)S(1)}, f32[1,16,2,256,128]{4,3,2,1,0:T(8,128)}) %tuple.78, ...), branch_computations={%region_3.3_spmd, %region_4.6_spmd} | conditional | flops 1092640768 | bytes 71827544 | solution.py:60
  97.1 14.2 %collective-permute-done = bf16[1,256,16,128]{3,1,2,0:T(8,128)(2,1)} collective-permute-done((bf16[1,256,16,128]{3,1,2,0:T(8,128)(2,1)}, bf16[1,256,16,128]{3,1,2,0:T(8,128)(2,1)}, u32[]{:S(2)}, u32[]{:S(2)}) %collective-permute-start) | collective-permute-done | bytes 1048608 | tf_op jit(solution)/shard_map/while/body/eval_jaxpr/ppermute | solution.py:58
  111.3 11.2 %collective-permute-done.1 = bf16[1,256,16,128]{3,1,2,0:T(8,128)(2,1)S(1)} collective-permute-done((bf16[1,256,16,128]{3,1,2,0:T(8,128)(2,1)}, bf16[1,256,16,128]{3,1,2,0:T(8,128)(2,1)S(1)}, u32[]{:S(2)}, u32[]{:S(2)}) %collective-permute-start.1) | collective-permute-done | bytes 1048608 | tf_op jit(solution)/shard_map/while/body/eval_jaxpr/ppermute | solution.py:59
  122.5 10.3 %conditional.4 = ((f32[1,16,2,256]{3,2,1,0:T(2,128)S(1)}, f32[1,16,2,256]{3,2,1,0:T(2,128)S(1)}, f32[1,16,2,256,128]{4,3,2,1,0:T(8,128)})) conditional(s32[]{:T(128)} %convert_element_type.100, (f32[1,16,2,256]{3,2,1,0:T(2,128)S(1)}, f32[1,16,2,256]{3,2,1,0:T(2,128)S(1)}, f32[1,16,2,256,128]{4,3,2,1,0:T(8,128)}) %tuple.78, ...), branch_computations={%region_3.3_spmd, %region_4.6_spmd} | conditional | flops 1092640768 | bytes 71827544 | solution.py:60
  136.2 14.2 %collective-permute-done = bf16[1,256,16,128]{3,1,2,0:T(8,128)(2,1)} collective-permute-done((bf16[1,256,16,128]{3,1,2,0:T(8,128)(2,1)}, bf16[1,256,16,128]{3,1,2,0:T(8,128)(2,1)}, u32[]{:S(2)}, u32[]{:S(2)}) %collective-permute-start) | collective-permute-done | bytes 1048608 | tf_op jit(solution)/shard_map/while/body/eval_jaxpr/ppermute | solution.py:58
  150.4 11.2 %collective-permute-done.1 = bf16[1,256,16,128]{3,1,2,0:T(8,128)(2,1)S(1)} collective-permute-done((bf16[1,256,16,128]{3,1,2,0:T(8,128)(2,1)}, bf16[1,256,16,128]{3,1,2,0:T(8,128)(2,1)S(1)}, u32[]{:S(2)}, u32[]{:S(2)}) %collective-permute-start.1) | collective-permute-done | bytes 1048608 | tf_op jit(solution)/shard_map/while/body/eval_jaxpr/ppermute | solution.py:59
  161.6 10.3 %conditional.4 = ((f32[1,16,2,256]{3,2,1,0:T(2,128)S(1)}, f32[1,16,2,256]{3,2,1,0:T(2,128)S(1)}, f32[1,16,2,256,128]{4,3,2,1,0:T(8,128)})) conditional(s32[]{:T(128)} %convert_element_type.100, (f32[1,16,2,256]{3,2,1,0:T(2,128)S(1)}, f32[1,16,2,256]{3,2,1,0:T(2,128)S(1)}, f32[1,16,2,256,128]{4,3,2,1,0:T(8,128)}) %tuple.78, ...), branch_computations={%region_3.3_spmd, %region_4.6_spmd} | conditional | flops 1092640768 | bytes 71827544 | solution.py:60
  175.2 14.2 %collective-permute-done = bf16[1,256,16,128]{3,1,2,0:T(8,128)(2,1)} collective-permute-done((bf16[1,256,16,128]{3,1,2,0:T(8,128)(2,1)}, bf16[1,256,16,128]{3,1,2,0:T(8,128)(2,1)}, u32[]{:S(2)}, u32[]{:S(2)}) %collective-permute-start) | collective-permute-done | bytes 1048608 | tf_op jit(solution)/shard_map/while/body/eval_jaxpr/ppermute | solution.py:58
  189.5 11.2 %collective-permute-done.1 = bf16[1,256,16,128]{3,1,2,0:T(8,128)(2,1)S(1)} collective-permute-done((bf16[1,256,16,128]{3,1,2,0:T(8,128)(2,1)}, bf16[1,256,16,128]{3,1,2,0:T(8,128)(2,1)S(1)}, u32[]{:S(2)}, u32[]{:S(2)}) %collective-permute-start.1) | collective-permute-done | bytes 1048608 | tf_op jit(solution)/shard_map/while/body/eval_jaxpr/ppermute | solution.py:59
  200.7 10.3 %conditional.4 = ((f32[1,16,2,256]{3,2,1,0:T(2,128)S(1)}, f32[1,16,2,256]{3,2,1,0:T(2,128)S(1)}, f32[1,16,2,256,128]{4,3,2,1,0:T(8,128)})) conditional(s32[]{:T(128)} %convert_element_type.100, (f32[1,16,2,256]{3,2,1,0:T(2,128)S(1)}, f32[1,16,2,256]{3,2,1,0:T(2,128)S(1)}, f32[1,16,2,256,128]{4,3,2,1,0:T(8,128)}) %tuple.78, ...), branch_computations={%region_3.3_spmd, %region_4.6_spmd} | conditional | flops 1092640768 | bytes 71827544 | solution.py:60
  214.3 14.2 %collective-permute-done = bf16[1,256,16,128]{3,1,2,0:T(8,128)(2,1)} collective-permute-done((bf16[1,256,16,128]{3,1,2,0:T(8,128)(2,1)}, bf16[1,256,16,128]{3,1,2,0:T(8,128)(2,1)}, u32[]{:S(2)}, u32[]{:S(2)}) %collective-permute-start) | collective-permute-done | bytes 1048608 | tf_op jit(solution)/shard_map/while/body/eval_jaxpr/ppermute | solution.py:58
  228.5 11.2 %collective-permute-done.1 = bf16[1,256,16,128]{3,1,2,0:T(8,128)(2,1)S(1)} collective-permute-done((bf16[1,256,16,128]{3,1,2,0:T(8,128)(2,1)}, bf16[1,256,16,128]{3,1,2,0:T(8,128)(2,1)S(1)}, u32[]{:S(2)}, u32[]{:S(2)}) %collective-permute-start.1) | collective-permute-done | bytes 1048608 | tf_op jit(solution)/shard_map/while/body/eval_jaxpr/ppermute | solution.py:59
  239.8 10.3 %conditional.4 = ((f32[1,16,2,256]{3,2,1,0:T(2,128)S(1)}, f32[1,16,2,256]{3,2,1,0:T(2,128)S(1)}, f32[1,16,2,256,128]{4,3,2,1,0:T(8,128)})) conditional(s32[]{:T(128)} %convert_element_type.100, (f32[1,16,2,256]{3,2,1,0:T(2,128)S(1)}, f32[1,16,2,256]{3,2,1,0:T(2,128)S(1)}, f32[1,16,2,256,128]{4,3,2,1,0:T(8,128)}) %tuple.78, ...), branch_computations={%region_3.3_spmd, %region_4.6_spmd} | conditional | flops 1092640768 | bytes 71827544 | solution.py:60
  253.4 14.2 %collective-permute-done = bf16[1,256,16,128]{3,1,2,0:T(8,128)(2,1)} collective-permute-done((bf16[1,256,16,128]{3,1,2,0:T(8,128)(2,1)}, bf16[1,256,16,128]{3,1,2,0:T(8,128)(2,1)}, u32[]{:S(2)}, u32[]{:S(2)}) %collective-permute-start) | collective-permute-done | bytes 1048608 | tf_op jit(solution)/shard_map/while/body/eval_jaxpr/ppermute | solution.py:58
  267.6 11.2 %collective-permute-done.1 = bf16[1,256,16,128]{3,1,2,0:T(8,128)(2,1)S(1)} collective-permute-done((bf16[1,256,16,128]{3,1,2,0:T(8,128)(2,1)}, bf16[1,256,16,128]{3,1,2,0:T(8,128)(2,1)S(1)}, u32[]{:S(2)}, u32[]{:S(2)}) %collective-permute-start.1) | collective-permute-done | bytes 1048608 | tf_op jit(solution)/shard_map/while/body/eval_jaxpr/ppermute | solution.py:59
  282.1 5.1 bitcast_convert_fusion
  287.2 7.5 multiply_reduce_fusion
  297.3 8.1 fusion.74
  305.3 5.8 fusion.54
  319.5 665.5 %while.43 = (s32[]{:T(128)}, bf16[1,256,16,128]{3,1,2,0:T(8,128)(2,1)}, bf16[1,256,16,128]{3,1,2,0:T(8,128)(2,1)}, f32[1,256,16,128]{3,1,2,0:T(8,128)}, f32[1,25...) while((s32[]{:T(128)}, ...), condition=%wide.region_11.12_spmd, body=%wide.region_8.11_spmd.sunk | while | flops 2704801792 | bytes 145850880 | solution.py:86
  319.6 59.1 %collective-permute-done.2 = bf16[1,256,16,128]{3,1,2,0:T(8,128)(2,1)S(1)} collective-permute-done((bf16[1,256,16,128]{3,1,2,0:T(8,128)(2,1)}, bf16[1,256,16,128]{3,1,2,0:T(8,128)(2,1)S(1)}, u32[]{:S(2)}, u32[]{:S(2)}) %collective-permute-start.2) | collective-permute-done | bytes 1048608 | tf_op jit(solution)/shard_map/while/body/eval_jaxpr/ppermute | solution.py:73
  379.7 10.2 %collective-permute-done.3 = bf16[1,256,16,128]{3,1,2,0:T(8,128)(2,1)} collective-permute-done((bf16[1,256,16,128]{3,1,2,0:T(8,128)(2,1)}, bf16[1,256,16,128]{3,1,2,0:T(8,128)(2,1)}, u32[]{:S(2)}, u32[]{:S(2)}) %collective-permute-start.3) | collective-permute-done | bytes 1048608 | tf_op jit(solution)/shard_map/while/body/eval_jaxpr/ppermute | solution.py:74
  392.2 18.8 %conditional.5 = ((f32[1,256,16,128]{3,1,2,0:T(8,128)}, f32[1,256,16,128]{3,1,2,0:T(8,128)}, f32[1,256,16,2,128]{4,1,3,2,0:T(8,128)})) conditional(s32[]{:T(128)} %convert_element_type.101, (f32[1,256,16,128]{3,1,2,0:T(8,128)}, f32[1,256,16,128]{3,1,2,0:T(8,128)}, f32[1,256,16,2,128]{4,1,3,2,0:T(8,128)}) %tuple.81, ...), branch_computations={%region_9.9_spmd, %region_10.10_spmd} | conditional | flops 2704801792 | bytes 108101752 | solution.py:83
  400.6 5.7 bitcast_add_fusion.4
  406.4 4.6 bitcast_add_fusion.3
  417.3 59.1 %collective-permute-done.2 = bf16[1,256,16,128]{3,1,2,0:T(8,128)(2,1)S(1)} collective-permute-done((bf16[1,256,16,128]{3,1,2,0:T(8,128)(2,1)}, bf16[1,256,16,128]{3,1,2,0:T(8,128)(2,1)S(1)}, u32[]{:S(2)}, u32[]{:S(2)}) %collective-permute-start.2) | collective-permute-done | bytes 1048608 | tf_op jit(solution)/shard_map/while/body/eval_jaxpr/ppermute | solution.py:73
  477.4 10.2 %collective-permute-done.3 = bf16[1,256,16,128]{3,1,2,0:T(8,128)(2,1)} collective-permute-done((bf16[1,256,16,128]{3,1,2,0:T(8,128)(2,1)}, bf16[1,256,16,128]{3,1,2,0:T(8,128)(2,1)}, u32[]{:S(2)}, u32[]{:S(2)}) %collective-permute-start.3) | collective-permute-done | bytes 1048608 | tf_op jit(solution)/shard_map/while/body/eval_jaxpr/ppermute | solution.py:74
  489.9 18.8 %conditional.5 = ((f32[1,256,16,128]{3,1,2,0:T(8,128)}, f32[1,256,16,128]{3,1,2,0:T(8,128)}, f32[1,256,16,2,128]{4,1,3,2,0:T(8,128)})) conditional(s32[]{:T(128)} %convert_element_type.101, (f32[1,256,16,128]{3,1,2,0:T(8,128)}, f32[1,256,16,128]{3,1,2,0:T(8,128)}, f32[1,256,16,2,128]{4,1,3,2,0:T(8,128)}) %tuple.81, ...), branch_computations={%region_9.9_spmd, %region_10.10_spmd} | conditional | flops 2704801792 | bytes 108101752 | solution.py:83
  491.5 3.7 fusion.23
  498.3 5.7 bitcast_add_fusion.4
  504.1 4.6 bitcast_add_fusion.3
  515.0 59.1 %collective-permute-done.2 = bf16[1,256,16,128]{3,1,2,0:T(8,128)(2,1)S(1)} collective-permute-done((bf16[1,256,16,128]{3,1,2,0:T(8,128)(2,1)}, bf16[1,256,16,128]{3,1,2,0:T(8,128)(2,1)S(1)}, u32[]{:S(2)}, u32[]{:S(2)}) %collective-permute-start.2) | collective-permute-done | bytes 1048608 | tf_op jit(solution)/shard_map/while/body/eval_jaxpr/ppermute | solution.py:73
  575.1 10.2 %collective-permute-done.3 = bf16[1,256,16,128]{3,1,2,0:T(8,128)(2,1)} collective-permute-done((bf16[1,256,16,128]{3,1,2,0:T(8,128)(2,1)}, bf16[1,256,16,128]{3,1,2,0:T(8,128)(2,1)}, u32[]{:S(2)}, u32[]{:S(2)}) %collective-permute-start.3) | collective-permute-done | bytes 1048608 | tf_op jit(solution)/shard_map/while/body/eval_jaxpr/ppermute | solution.py:74
  587.6 18.8 %conditional.5 = ((f32[1,256,16,128]{3,1,2,0:T(8,128)}, f32[1,256,16,128]{3,1,2,0:T(8,128)}, f32[1,256,16,2,128]{4,1,3,2,0:T(8,128)})) conditional(s32[]{:T(128)} %convert_element_type.101, (f32[1,256,16,128]{3,1,2,0:T(8,128)}, f32[1,256,16,128]{3,1,2,0:T(8,128)}, f32[1,256,16,2,128]{4,1,3,2,0:T(8,128)}) %tuple.81, ...), branch_computations={%region_9.9_spmd, %region_10.10_spmd} | conditional | flops 2704801792 | bytes 108101752 | solution.py:83
  589.2 3.7 fusion.23
  596.1 5.7 bitcast_add_fusion.4
  601.8 4.6 bitcast_add_fusion.3
  612.8 59.1 %collective-permute-done.2 = bf16[1,256,16,128]{3,1,2,0:T(8,128)(2,1)S(1)} collective-permute-done((bf16[1,256,16,128]{3,1,2,0:T(8,128)(2,1)}, bf16[1,256,16,128]{3,1,2,0:T(8,128)(2,1)S(1)}, u32[]{:S(2)}, u32[]{:S(2)}) %collective-permute-start.2) | collective-permute-done | bytes 1048608 | tf_op jit(solution)/shard_map/while/body/eval_jaxpr/ppermute | solution.py:73
  672.8 10.2 %collective-permute-done.3 = bf16[1,256,16,128]{3,1,2,0:T(8,128)(2,1)} collective-permute-done((bf16[1,256,16,128]{3,1,2,0:T(8,128)(2,1)}, bf16[1,256,16,128]{3,1,2,0:T(8,128)(2,1)}, u32[]{:S(2)}, u32[]{:S(2)}) %collective-permute-start.3) | collective-permute-done | bytes 1048608 | tf_op jit(solution)/shard_map/while/body/eval_jaxpr/ppermute | solution.py:74
  685.4 18.8 %conditional.5 = ((f32[1,256,16,128]{3,1,2,0:T(8,128)}, f32[1,256,16,128]{3,1,2,0:T(8,128)}, f32[1,256,16,2,128]{4,1,3,2,0:T(8,128)})) conditional(s32[]{:T(128)} %convert_element_type.101, (f32[1,256,16,128]{3,1,2,0:T(8,128)}, f32[1,256,16,128]{3,1,2,0:T(8,128)}, f32[1,256,16,2,128]{4,1,3,2,0:T(8,128)}) %tuple.81, ...), branch_computations={%region_9.9_spmd, %region_10.10_spmd} | conditional | flops 2704801792 | bytes 108101752 | solution.py:83
  687.0 3.7 fusion.23
  693.8 5.7 bitcast_add_fusion.4
  699.5 4.6 bitcast_add_fusion.3
  710.5 59.1 %collective-permute-done.2 = bf16[1,256,16,128]{3,1,2,0:T(8,128)(2,1)S(1)} collective-permute-done((bf16[1,256,16,128]{3,1,2,0:T(8,128)(2,1)}, bf16[1,256,16,128]{3,1,2,0:T(8,128)(2,1)S(1)}, u32[]{:S(2)}, u32[]{:S(2)}) %collective-permute-start.2) | collective-permute-done | bytes 1048608 | tf_op jit(solution)/shard_map/while/body/eval_jaxpr/ppermute | solution.py:73
  770.6 10.2 %collective-permute-done.3 = bf16[1,256,16,128]{3,1,2,0:T(8,128)(2,1)} collective-permute-done((bf16[1,256,16,128]{3,1,2,0:T(8,128)(2,1)}, bf16[1,256,16,128]{3,1,2,0:T(8,128)(2,1)}, u32[]{:S(2)}, u32[]{:S(2)}) %collective-permute-start.3) | collective-permute-done | bytes 1048608 | tf_op jit(solution)/shard_map/while/body/eval_jaxpr/ppermute | solution.py:74
  783.1 18.8 %conditional.5 = ((f32[1,256,16,128]{3,1,2,0:T(8,128)}, f32[1,256,16,128]{3,1,2,0:T(8,128)}, f32[1,256,16,2,128]{4,1,3,2,0:T(8,128)})) conditional(s32[]{:T(128)} %convert_element_type.101, (f32[1,256,16,128]{3,1,2,0:T(8,128)}, f32[1,256,16,128]{3,1,2,0:T(8,128)}, f32[1,256,16,2,128]{4,1,3,2,0:T(8,128)}) %tuple.81, ...), branch_computations={%region_9.9_spmd, %region_10.10_spmd} | conditional | flops 2704801792 | bytes 108101752 | solution.py:83
  784.7 3.7 fusion.23
  791.5 5.7 bitcast_add_fusion.4
  797.2 4.6 bitcast_add_fusion.3
  808.2 59.1 %collective-permute-done.2 = bf16[1,256,16,128]{3,1,2,0:T(8,128)(2,1)S(1)} collective-permute-done((bf16[1,256,16,128]{3,1,2,0:T(8,128)(2,1)}, bf16[1,256,16,128]{3,1,2,0:T(8,128)(2,1)S(1)}, u32[]{:S(2)}, u32[]{:S(2)}) %collective-permute-start.2) | collective-permute-done | bytes 1048608 | tf_op jit(solution)/shard_map/while/body/eval_jaxpr/ppermute | solution.py:73
  868.3 10.2 %collective-permute-done.3 = bf16[1,256,16,128]{3,1,2,0:T(8,128)(2,1)} collective-permute-done((bf16[1,256,16,128]{3,1,2,0:T(8,128)(2,1)}, bf16[1,256,16,128]{3,1,2,0:T(8,128)(2,1)}, u32[]{:S(2)}, u32[]{:S(2)}) %collective-permute-start.3) | collective-permute-done | bytes 1048608 | tf_op jit(solution)/shard_map/while/body/eval_jaxpr/ppermute | solution.py:74
  880.8 18.8 %conditional.5 = ((f32[1,256,16,128]{3,1,2,0:T(8,128)}, f32[1,256,16,128]{3,1,2,0:T(8,128)}, f32[1,256,16,2,128]{4,1,3,2,0:T(8,128)})) conditional(s32[]{:T(128)} %convert_element_type.101, (f32[1,256,16,128]{3,1,2,0:T(8,128)}, f32[1,256,16,128]{3,1,2,0:T(8,128)}, f32[1,256,16,2,128]{4,1,3,2,0:T(8,128)}) %tuple.81, ...), branch_computations={%region_9.9_spmd, %region_10.10_spmd} | conditional | flops 2704801792 | bytes 108101752 | solution.py:83
  889.2 5.7 bitcast_add_fusion.4
  895.0 4.6 bitcast_add_fusion.3
  905.9 59.1 %collective-permute-done.2 = bf16[1,256,16,128]{3,1,2,0:T(8,128)(2,1)S(1)} collective-permute-done((bf16[1,256,16,128]{3,1,2,0:T(8,128)(2,1)}, bf16[1,256,16,128]{3,1,2,0:T(8,128)(2,1)S(1)}, u32[]{:S(2)}, u32[]{:S(2)}) %collective-permute-start.2) | collective-permute-done | bytes 1048608 | tf_op jit(solution)/shard_map/while/body/eval_jaxpr/ppermute | solution.py:73
  966.0 10.2 %collective-permute-done.3 = bf16[1,256,16,128]{3,1,2,0:T(8,128)(2,1)} collective-permute-done((bf16[1,256,16,128]{3,1,2,0:T(8,128)(2,1)}, bf16[1,256,16,128]{3,1,2,0:T(8,128)(2,1)}, u32[]{:S(2)}, u32[]{:S(2)}) %collective-permute-start.3) | collective-permute-done | bytes 1048608 | tf_op jit(solution)/shard_map/while/body/eval_jaxpr/ppermute | solution.py:74
  1002.2 11.2 %collective-permute-done.7 = bf16[1,256,16,128]{3,2,1,0:T(8,128)(2,1)} collective-permute-done((bf16[1,256,16,128]{3,2,1,0:T(8,128)(2,1)S(1)}, bf16[1,256,16,128]{3,2,1,0:T(8,128)(2,1)}, u32[]{:S(2)}, u32[]{:S(2)}) %collective-permute-start.7) | collective-permute-done | bytes 1048608 | tf_op jit(solution)/shard_map/ppermute | solution.py:88
  (260 shorter events, 230.2 us)
Async XLA Ops:
  3.6 7.0 copy-start.10
  5.9 3.3 copy-start.6
  9.5 9.4 copy-start.11
  19.0 14.2 %collective-permute-start = (bf16[1,256,16,128]{3,1,2,0:T(8,128)(2,1)}, bf16[1,256,16,128]{3,1,2,0:T(8,128)(2,1)}, u32[]{:S(2)}, u32[]{:S(2)}) collective-permute-start(bf16[1,256,16,128]{3,1,2,0:T(8,128)(2,1)} %get-tuple-element.628), channel_id=1, source_target_pairs={{0,1},{1,2},{2,3},{3,4},{4,5},{5,6},{6,7},{7,0},{8,9},{9,10},{10,1... | collective-permute-start | bytes 3145736 | tf_op jit(solution)/shard_map/while/body/eval_jaxpr/ppermute | solution.py:58
  19.0 25.5 %collective-permute-start.1 = (bf16[1,256,16,128]{3,1,2,0:T(8,128)(2,1)}, bf16[1,256,16,128]{3,1,2,0:T(8,128)(2,1)S(1)}, u32[]{:S(2)}, u32[]{:S(2)}) collective-permute-start(bf16[1,256,16,128]{3,1,2,0:T(8,128)(2,1)} %get-tuple-element.629), channel_id=1, source_target_pairs={{0,1},{1,2},{2,3},{3,4},{4,5},{5,6},{6,7},{7,0},{8,9},{9,10},{10,1... | collective-permute-start | bytes 3145736 | tf_op jit(solution)/shard_map/while/body/eval_jaxpr/ppermute | solution.py:59
  58.0 14.2 %collective-permute-start = (bf16[1,256,16,128]{3,1,2,0:T(8,128)(2,1)}, bf16[1,256,16,128]{3,1,2,0:T(8,128)(2,1)}, u32[]{:S(2)}, u32[]{:S(2)}) collective-permute-start(bf16[1,256,16,128]{3,1,2,0:T(8,128)(2,1)} %get-tuple-element.628), channel_id=1, source_target_pairs={{0,1},{1,2},{2,3},{3,4},{4,5},{5,6},{6,7},{7,0},{8,9},{9,10},{10,1... | collective-permute-start | bytes 3145736 | tf_op jit(solution)/shard_map/while/body/eval_jaxpr/ppermute | solution.py:58
  58.0 25.5 %collective-permute-start.1 = (bf16[1,256,16,128]{3,1,2,0:T(8,128)(2,1)}, bf16[1,256,16,128]{3,1,2,0:T(8,128)(2,1)S(1)}, u32[]{:S(2)}, u32[]{:S(2)}) collective-permute-start(bf16[1,256,16,128]{3,1,2,0:T(8,128)(2,1)} %get-tuple-element.629), channel_id=1, source_target_pairs={{0,1},{1,2},{2,3},{3,4},{4,5},{5,6},{6,7},{7,0},{8,9},{9,10},{10,1... | collective-permute-start | bytes 3145736 | tf_op jit(solution)/shard_map/while/body/eval_jaxpr/ppermute | solution.py:59
  97.1 14.2 %collective-permute-start = (bf16[1,256,16,128]{3,1,2,0:T(8,128)(2,1)}, bf16[1,256,16,128]{3,1,2,0:T(8,128)(2,1)}, u32[]{:S(2)}, u32[]{:S(2)}) collective-permute-start(bf16[1,256,16,128]{3,1,2,0:T(8,128)(2,1)} %get-tuple-element.628), channel_id=1, source_target_pairs={{0,1},{1,2},{2,3},{3,4},{4,5},{5,6},{6,7},{7,0},{8,9},{9,10},{10,1... | collective-permute-start | bytes 3145736 | tf_op jit(solution)/shard_map/while/body/eval_jaxpr/ppermute | solution.py:58
  97.1 25.5 %collective-permute-start.1 = (bf16[1,256,16,128]{3,1,2,0:T(8,128)(2,1)}, bf16[1,256,16,128]{3,1,2,0:T(8,128)(2,1)S(1)}, u32[]{:S(2)}, u32[]{:S(2)}) collective-permute-start(bf16[1,256,16,128]{3,1,2,0:T(8,128)(2,1)} %get-tuple-element.629), channel_id=1, source_target_pairs={{0,1},{1,2},{2,3},{3,4},{4,5},{5,6},{6,7},{7,0},{8,9},{9,10},{10,1... | collective-permute-start | bytes 3145736 | tf_op jit(solution)/shard_map/while/body/eval_jaxpr/ppermute | solution.py:59
  136.2 14.2 %collective-permute-start = (bf16[1,256,16,128]{3,1,2,0:T(8,128)(2,1)}, bf16[1,256,16,128]{3,1,2,0:T(8,128)(2,1)}, u32[]{:S(2)}, u32[]{:S(2)}) collective-permute-start(bf16[1,256,16,128]{3,1,2,0:T(8,128)(2,1)} %get-tuple-element.628), channel_id=1, source_target_pairs={{0,1},{1,2},{2,3},{3,4},{4,5},{5,6},{6,7},{7,0},{8,9},{9,10},{10,1... | collective-permute-start | bytes 3145736 | tf_op jit(solution)/shard_map/while/body/eval_jaxpr/ppermute | solution.py:58
  136.2 25.5 %collective-permute-start.1 = (bf16[1,256,16,128]{3,1,2,0:T(8,128)(2,1)}, bf16[1,256,16,128]{3,1,2,0:T(8,128)(2,1)S(1)}, u32[]{:S(2)}, u32[]{:S(2)}) collective-permute-start(bf16[1,256,16,128]{3,1,2,0:T(8,128)(2,1)} %get-tuple-element.629), channel_id=1, source_target_pairs={{0,1},{1,2},{2,3},{3,4},{4,5},{5,6},{6,7},{7,0},{8,9},{9,10},{10,1... | collective-permute-start | bytes 3145736 | tf_op jit(solution)/shard_map/while/body/eval_jaxpr/ppermute | solution.py:59
  175.2 14.2 %collective-permute-start = (bf16[1,256,16,128]{3,1,2,0:T(8,128)(2,1)}, bf16[1,256,16,128]{3,1,2,0:T(8,128)(2,1)}, u32[]{:S(2)}, u32[]{:S(2)}) collective-permute-start(bf16[1,256,16,128]{3,1,2,0:T(8,128)(2,1)} %get-tuple-element.628), channel_id=1, source_target_pairs={{0,1},{1,2},{2,3},{3,4},{4,5},{5,6},{6,7},{7,0},{8,9},{9,10},{10,1... | collective-permute-start | bytes 3145736 | tf_op jit(solution)/shard_map/while/body/eval_jaxpr/ppermute | solution.py:58
  175.2 25.5 %collective-permute-start.1 = (bf16[1,256,16,128]{3,1,2,0:T(8,128)(2,1)}, bf16[1,256,16,128]{3,1,2,0:T(8,128)(2,1)S(1)}, u32[]{:S(2)}, u32[]{:S(2)}) collective-permute-start(bf16[1,256,16,128]{3,1,2,0:T(8,128)(2,1)} %get-tuple-element.629), channel_id=1, source_target_pairs={{0,1},{1,2},{2,3},{3,4},{4,5},{5,6},{6,7},{7,0},{8,9},{9,10},{10,1... | collective-permute-start | bytes 3145736 | tf_op jit(solution)/shard_map/while/body/eval_jaxpr/ppermute | solution.py:59
  214.3 14.2 %collective-permute-start = (bf16[1,256,16,128]{3,1,2,0:T(8,128)(2,1)}, bf16[1,256,16,128]{3,1,2,0:T(8,128)(2,1)}, u32[]{:S(2)}, u32[]{:S(2)}) collective-permute-start(bf16[1,256,16,128]{3,1,2,0:T(8,128)(2,1)} %get-tuple-element.628), channel_id=1, source_target_pairs={{0,1},{1,2},{2,3},{3,4},{4,5},{5,6},{6,7},{7,0},{8,9},{9,10},{10,1... | collective-permute-start | bytes 3145736 | tf_op jit(solution)/shard_map/while/body/eval_jaxpr/ppermute | solution.py:58
  214.3 25.5 %collective-permute-start.1 = (bf16[1,256,16,128]{3,1,2,0:T(8,128)(2,1)}, bf16[1,256,16,128]{3,1,2,0:T(8,128)(2,1)S(1)}, u32[]{:S(2)}, u32[]{:S(2)}) collective-permute-start(bf16[1,256,16,128]{3,1,2,0:T(8,128)(2,1)} %get-tuple-element.629), channel_id=1, source_target_pairs={{0,1},{1,2},{2,3},{3,4},{4,5},{5,6},{6,7},{7,0},{8,9},{9,10},{10,1... | collective-permute-start | bytes 3145736 | tf_op jit(solution)/shard_map/while/body/eval_jaxpr/ppermute | solution.py:59
  253.4 14.2 %collective-permute-start = (bf16[1,256,16,128]{3,1,2,0:T(8,128)(2,1)}, bf16[1,256,16,128]{3,1,2,0:T(8,128)(2,1)}, u32[]{:S(2)}, u32[]{:S(2)}) collective-permute-start(bf16[1,256,16,128]{3,1,2,0:T(8,128)(2,1)} %get-tuple-element.628), channel_id=1, source_target_pairs={{0,1},{1,2},{2,3},{3,4},{4,5},{5,6},{6,7},{7,0},{8,9},{9,10},{10,1... | collective-permute-start | bytes 3145736 | tf_op jit(solution)/shard_map/while/body/eval_jaxpr/ppermute | solution.py:58
  253.4 25.5 %collective-permute-start.1 = (bf16[1,256,16,128]{3,1,2,0:T(8,128)(2,1)}, bf16[1,256,16,128]{3,1,2,0:T(8,128)(2,1)S(1)}, u32[]{:S(2)}, u32[]{:S(2)}) collective-permute-start(bf16[1,256,16,128]{3,1,2,0:T(8,128)(2,1)} %get-tuple-element.629), channel_id=1, source_target_pairs={{0,1},{1,2},{2,3},{3,4},{4,5},{5,6},{6,7},{7,0},{8,9},{9,10},{10,1... | collective-permute-start | bytes 3145736 | tf_op jit(solution)/shard_map/while/body/eval_jaxpr/ppermute | solution.py:59
  297.2 8.1 copy-start.7
  297.3 8.1 copy-start.16
  305.3 5.8 copy-start.9
  311.2 3.4 copy-start.14
  319.5 72.7 %collective-permute-start.4 = (f32[1,256,16,128]{3,1,2,0:T(8,128)}, f32[1,256,16,128]{3,1,2,0:T(8,128)}, u32[]{:S(2)}, u32[]{:S(2)}) collective-permute-start(f32[1,256,16,128]{3,1,2,0:T(8,128)} %get-tuple-element.660), channel_id=1, source_target_pairs={{0,1},{1,2},{2,3},{3,4},{4,5},{5,6},{6,7},{7,0},{8,9},{9,10},{10,1... | collective-permute-start | bytes 6291464 | tf_op jit(solution)/shard_map/while/body/eval_jaxpr/ppermute | solution.py:75
  319.5 72.7 %collective-permute-start.5 = (f32[1,256,16,128]{3,1,2,0:T(8,128)}, f32[1,256,16,128]{3,1,2,0:T(8,128)}, u32[]{:S(2)}, u32[]{:S(2)}) collective-permute-start(f32[1,256,16,128]{3,1,2,0:T(8,128)} %get-tuple-element.661), channel_id=1, source_target_pairs={{0,1},{1,2},{2,3},{3,4},{4,5},{5,6},{6,7},{7,0},{8,9},{9,10},{10,1... | collective-permute-start | bytes 6291464 | tf_op jit(solution)/shard_map/while/body/eval_jaxpr/ppermute | solution.py:76
  319.5 59.2 %collective-permute-start.2 = (bf16[1,256,16,128]{3,1,2,0:T(8,128)(2,1)}, bf16[1,256,16,128]{3,1,2,0:T(8,128)(2,1)S(1)}, u32[]{:S(2)}, u32[]{:S(2)}) collective-permute-start(bf16[1,256,16,128]{3,1,2,0:T(8,128)(2,1)} %get-tuple-element.658), channel_id=1, source_target_pairs={{0,1},{1,2},{2,3},{3,4},{4,5},{5,6},{6,7},{7,0},{8,9},{9,10},{10,1... | collective-permute-start | bytes 3145736 | tf_op jit(solution)/shard_map/while/body/eval_jaxpr/ppermute | solution.py:73
  319.5 70.4 %collective-permute-start.3 = (bf16[1,256,16,128]{3,1,2,0:T(8,128)(2,1)}, bf16[1,256,16,128]{3,1,2,0:T(8,128)(2,1)}, u32[]{:S(2)}, u32[]{:S(2)}) collective-permute-start(bf16[1,256,16,128]{3,1,2,0:T(8,128)(2,1)} %get-tuple-element.659), channel_id=1, source_target_pairs={{0,1},{1,2},{2,3},{3,4},{4,5},{5,6},{6,7},{7,0},{8,9},{9,10},{10,1... | collective-permute-start | bytes 3145736 | tf_op jit(solution)/shard_map/while/body/eval_jaxpr/ppermute | solution.py:74
  393.8 3.7 copy-start.1
  400.6 5.8 copy-start.2
  417.2 72.7 %collective-permute-start.4 = (f32[1,256,16,128]{3,1,2,0:T(8,128)}, f32[1,256,16,128]{3,1,2,0:T(8,128)}, u32[]{:S(2)}, u32[]{:S(2)}) collective-permute-start(f32[1,256,16,128]{3,1,2,0:T(8,128)} %get-tuple-element.660), channel_id=1, source_target_pairs={{0,1},{1,2},{2,3},{3,4},{4,5},{5,6},{6,7},{7,0},{8,9},{9,10},{10,1... | collective-permute-start | bytes 6291464 | tf_op jit(solution)/shard_map/while/body/eval_jaxpr/ppermute | solution.py:75
  417.2 72.7 %collective-permute-start.5 = (f32[1,256,16,128]{3,1,2,0:T(8,128)}, f32[1,256,16,128]{3,1,2,0:T(8,128)}, u32[]{:S(2)}, u32[]{:S(2)}) collective-permute-start(f32[1,256,16,128]{3,1,2,0:T(8,128)} %get-tuple-element.661), channel_id=1, source_target_pairs={{0,1},{1,2},{2,3},{3,4},{4,5},{5,6},{6,7},{7,0},{8,9},{9,10},{10,1... | collective-permute-start | bytes 6291464 | tf_op jit(solution)/shard_map/while/body/eval_jaxpr/ppermute | solution.py:76
  417.2 59.2 %collective-permute-start.2 = (bf16[1,256,16,128]{3,1,2,0:T(8,128)(2,1)}, bf16[1,256,16,128]{3,1,2,0:T(8,128)(2,1)S(1)}, u32[]{:S(2)}, u32[]{:S(2)}) collective-permute-start(bf16[1,256,16,128]{3,1,2,0:T(8,128)(2,1)} %get-tuple-element.658), channel_id=1, source_target_pairs={{0,1},{1,2},{2,3},{3,4},{4,5},{5,6},{6,7},{7,0},{8,9},{9,10},{10,1... | collective-permute-start | bytes 3145736 | tf_op jit(solution)/shard_map/while/body/eval_jaxpr/ppermute | solution.py:73
  417.2 70.4 %collective-permute-start.3 = (bf16[1,256,16,128]{3,1,2,0:T(8,128)(2,1)}, bf16[1,256,16,128]{3,1,2,0:T(8,128)(2,1)}, u32[]{:S(2)}, u32[]{:S(2)}) collective-permute-start(bf16[1,256,16,128]{3,1,2,0:T(8,128)(2,1)} %get-tuple-element.659), channel_id=1, source_target_pairs={{0,1},{1,2},{2,3},{3,4},{4,5},{5,6},{6,7},{7,0},{8,9},{9,10},{10,1... | collective-permute-start | bytes 3145736 | tf_op jit(solution)/shard_map/while/body/eval_jaxpr/ppermute | solution.py:74
  491.5 3.7 copy-start.1
  498.3 5.8 copy-start.2
  514.9 72.7 %collective-permute-start.4 = (f32[1,256,16,128]{3,1,2,0:T(8,128)}, f32[1,256,16,128]{3,1,2,0:T(8,128)}, u32[]{:S(2)}, u32[]{:S(2)}) collective-permute-start(f32[1,256,16,128]{3,1,2,0:T(8,128)} %get-tuple-element.660), channel_id=1, source_target_pairs={{0,1},{1,2},{2,3},{3,4},{4,5},{5,6},{6,7},{7,0},{8,9},{9,10},{10,1... | collective-permute-start | bytes 6291464 | tf_op jit(solution)/shard_map/while/body/eval_jaxpr/ppermute | solution.py:75
  514.9 72.7 %collective-permute-start.5 = (f32[1,256,16,128]{3,1,2,0:T(8,128)}, f32[1,256,16,128]{3,1,2,0:T(8,128)}, u32[]{:S(2)}, u32[]{:S(2)}) collective-permute-start(f32[1,256,16,128]{3,1,2,0:T(8,128)} %get-tuple-element.661), channel_id=1, source_target_pairs={{0,1},{1,2},{2,3},{3,4},{4,5},{5,6},{6,7},{7,0},{8,9},{9,10},{10,1... | collective-permute-start | bytes 6291464 | tf_op jit(solution)/shard_map/while/body/eval_jaxpr/ppermute | solution.py:76
  514.9 59.2 %collective-permute-start.2 = (bf16[1,256,16,128]{3,1,2,0:T(8,128)(2,1)}, bf16[1,256,16,128]{3,1,2,0:T(8,128)(2,1)S(1)}, u32[]{:S(2)}, u32[]{:S(2)}) collective-permute-start(bf16[1,256,16,128]{3,1,2,0:T(8,128)(2,1)} %get-tuple-element.658), channel_id=1, source_target_pairs={{0,1},{1,2},{2,3},{3,4},{4,5},{5,6},{6,7},{7,0},{8,9},{9,10},{10,1... | collective-permute-start | bytes 3145736 | tf_op jit(solution)/shard_map/while/body/eval_jaxpr/ppermute | solution.py:73
  515.0 70.4 %collective-permute-start.3 = (bf16[1,256,16,128]{3,1,2,0:T(8,128)(2,1)}, bf16[1,256,16,128]{3,1,2,0:T(8,128)(2,1)}, u32[]{:S(2)}, u32[]{:S(2)}) collective-permute-start(bf16[1,256,16,128]{3,1,2,0:T(8,128)(2,1)} %get-tuple-element.659), channel_id=1, source_target_pairs={{0,1},{1,2},{2,3},{3,4},{4,5},{5,6},{6,7},{7,0},{8,9},{9,10},{10,1... | collective-permute-start | bytes 3145736 | tf_op jit(solution)/shard_map/while/body/eval_jaxpr/ppermute | solution.py:74
  589.2 3.7 copy-start.1
  596.1 5.8 copy-start.2
  612.6 72.7 %collective-permute-start.4 = (f32[1,256,16,128]{3,1,2,0:T(8,128)}, f32[1,256,16,128]{3,1,2,0:T(8,128)}, u32[]{:S(2)}, u32[]{:S(2)}) collective-permute-start(f32[1,256,16,128]{3,1,2,0:T(8,128)} %get-tuple-element.660), channel_id=1, source_target_pairs={{0,1},{1,2},{2,3},{3,4},{4,5},{5,6},{6,7},{7,0},{8,9},{9,10},{10,1... | collective-permute-start | bytes 6291464 | tf_op jit(solution)/shard_map/while/body/eval_jaxpr/ppermute | solution.py:75
  612.6 72.7 %collective-permute-start.5 = (f32[1,256,16,128]{3,1,2,0:T(8,128)}, f32[1,256,16,128]{3,1,2,0:T(8,128)}, u32[]{:S(2)}, u32[]{:S(2)}) collective-permute-start(f32[1,256,16,128]{3,1,2,0:T(8,128)} %get-tuple-element.661), channel_id=1, source_target_pairs={{0,1},{1,2},{2,3},{3,4},{4,5},{5,6},{6,7},{7,0},{8,9},{9,10},{10,1... | collective-permute-start | bytes 6291464 | tf_op jit(solution)/shard_map/while/body/eval_jaxpr/ppermute | solution.py:76
  612.7 59.2 %collective-permute-start.2 = (bf16[1,256,16,128]{3,1,2,0:T(8,128)(2,1)}, bf16[1,256,16,128]{3,1,2,0:T(8,128)(2,1)S(1)}, u32[]{:S(2)}, u32[]{:S(2)}) collective-permute-start(bf16[1,256,16,128]{3,1,2,0:T(8,128)(2,1)} %get-tuple-element.658), channel_id=1, source_target_pairs={{0,1},{1,2},{2,3},{3,4},{4,5},{5,6},{6,7},{7,0},{8,9},{9,10},{10,1... | collective-permute-start | bytes 3145736 | tf_op jit(solution)/shard_map/while/body/eval_jaxpr/ppermute | solution.py:73
  612.7 70.4 %collective-permute-start.3 = (bf16[1,256,16,128]{3,1,2,0:T(8,128)(2,1)}, bf16[1,256,16,128]{3,1,2,0:T(8,128)(2,1)}, u32[]{:S(2)}, u32[]{:S(2)}) collective-permute-start(bf16[1,256,16,128]{3,1,2,0:T(8,128)(2,1)} %get-tuple-element.659), channel_id=1, source_target_pairs={{0,1},{1,2},{2,3},{3,4},{4,5},{5,6},{6,7},{7,0},{8,9},{9,10},{10,1... | collective-permute-start | bytes 3145736 | tf_op jit(solution)/shard_map/while/body/eval_jaxpr/ppermute | solution.py:74
  687.0 3.7 copy-start.1
  693.8 5.8 copy-start.2
  710.4 72.7 %collective-permute-start.4 = (f32[1,256,16,128]{3,1,2,0:T(8,128)}, f32[1,256,16,128]{3,1,2,0:T(8,128)}, u32[]{:S(2)}, u32[]{:S(2)}) collective-permute-start(f32[1,256,16,128]{3,1,2,0:T(8,128)} %get-tuple-element.660), channel_id=1, source_target_pairs={{0,1},{1,2},{2,3},{3,4},{4,5},{5,6},{6,7},{7,0},{8,9},{9,10},{10,1... | collective-permute-start | bytes 6291464 | tf_op jit(solution)/shard_map/while/body/eval_jaxpr/ppermute | solution.py:75
  710.4 72.7 %collective-permute-start.5 = (f32[1,256,16,128]{3,1,2,0:T(8,128)}, f32[1,256,16,128]{3,1,2,0:T(8,128)}, u32[]{:S(2)}, u32[]{:S(2)}) collective-permute-start(f32[1,256,16,128]{3,1,2,0:T(8,128)} %get-tuple-element.661), channel_id=1, source_target_pairs={{0,1},{1,2},{2,3},{3,4},{4,5},{5,6},{6,7},{7,0},{8,9},{9,10},{10,1... | collective-permute-start | bytes 6291464 | tf_op jit(solution)/shard_map/while/body/eval_jaxpr/ppermute | solution.py:76
  710.4 59.2 %collective-permute-start.2 = (bf16[1,256,16,128]{3,1,2,0:T(8,128)(2,1)}, bf16[1,256,16,128]{3,1,2,0:T(8,128)(2,1)S(1)}, u32[]{:S(2)}, u32[]{:S(2)}) collective-permute-start(bf16[1,256,16,128]{3,1,2,0:T(8,128)(2,1)} %get-tuple-element.658), channel_id=1, source_target_pairs={{0,1},{1,2},{2,3},{3,4},{4,5},{5,6},{6,7},{7,0},{8,9},{9,10},{10,1... | collective-permute-start | bytes 3145736 | tf_op jit(solution)/shard_map/while/body/eval_jaxpr/ppermute | solution.py:73
  710.4 70.4 %collective-permute-start.3 = (bf16[1,256,16,128]{3,1,2,0:T(8,128)(2,1)}, bf16[1,256,16,128]{3,1,2,0:T(8,128)(2,1)}, u32[]{:S(2)}, u32[]{:S(2)}) collective-permute-start(bf16[1,256,16,128]{3,1,2,0:T(8,128)(2,1)} %get-tuple-element.659), channel_id=1, source_target_pairs={{0,1},{1,2},{2,3},{3,4},{4,5},{5,6},{6,7},{7,0},{8,9},{9,10},{10,1... | collective-permute-start | bytes 3145736 | tf_op jit(solution)/shard_map/while/body/eval_jaxpr/ppermute | solution.py:74
  784.7 3.7 copy-start.1
  791.5 5.8 copy-start.2
  808.1 72.7 %collective-permute-start.4 = (f32[1,256,16,128]{3,1,2,0:T(8,128)}, f32[1,256,16,128]{3,1,2,0:T(8,128)}, u32[]{:S(2)}, u32[]{:S(2)}) collective-permute-start(f32[1,256,16,128]{3,1,2,0:T(8,128)} %get-tuple-element.660), channel_id=1, source_target_pairs={{0,1},{1,2},{2,3},{3,4},{4,5},{5,6},{6,7},{7,0},{8,9},{9,10},{10,1... | collective-permute-start | bytes 6291464 | tf_op jit(solution)/shard_map/while/body/eval_jaxpr/ppermute | solution.py:75
  808.1 72.7 %collective-permute-start.5 = (f32[1,256,16,128]{3,1,2,0:T(8,128)}, f32[1,256,16,128]{3,1,2,0:T(8,128)}, u32[]{:S(2)}, u32[]{:S(2)}) collective-permute-start(f32[1,256,16,128]{3,1,2,0:T(8,128)} %get-tuple-element.661), channel_id=1, source_target_pairs={{0,1},{1,2},{2,3},{3,4},{4,5},{5,6},{6,7},{7,0},{8,9},{9,10},{10,1... | collective-permute-start | bytes 6291464 | tf_op jit(solution)/shard_map/while/body/eval_jaxpr/ppermute | solution.py:76
  808.1 59.2 %collective-permute-start.2 = (bf16[1,256,16,128]{3,1,2,0:T(8,128)(2,1)}, bf16[1,256,16,128]{3,1,2,0:T(8,128)(2,1)S(1)}, u32[]{:S(2)}, u32[]{:S(2)}) collective-permute-start(bf16[1,256,16,128]{3,1,2,0:T(8,128)(2,1)} %get-tuple-element.658), channel_id=1, source_target_pairs={{0,1},{1,2},{2,3},{3,4},{4,5},{5,6},{6,7},{7,0},{8,9},{9,10},{10,1... | collective-permute-start | bytes 3145736 | tf_op jit(solution)/shard_map/while/body/eval_jaxpr/ppermute | solution.py:73
  808.1 70.4 %collective-permute-start.3 = (bf16[1,256,16,128]{3,1,2,0:T(8,128)(2,1)}, bf16[1,256,16,128]{3,1,2,0:T(8,128)(2,1)}, u32[]{:S(2)}, u32[]{:S(2)}) collective-permute-start(bf16[1,256,16,128]{3,1,2,0:T(8,128)(2,1)} %get-tuple-element.659), channel_id=1, source_target_pairs={{0,1},{1,2},{2,3},{3,4},{4,5},{5,6},{6,7},{7,0},{8,9},{9,10},{10,1... | collective-permute-start | bytes 3145736 | tf_op jit(solution)/shard_map/while/body/eval_jaxpr/ppermute | solution.py:74
  882.4 3.7 copy-start.1
  889.2 5.8 copy-start.2
  905.8 72.7 %collective-permute-start.4 = (f32[1,256,16,128]{3,1,2,0:T(8,128)}, f32[1,256,16,128]{3,1,2,0:T(8,128)}, u32[]{:S(2)}, u32[]{:S(2)}) collective-permute-start(f32[1,256,16,128]{3,1,2,0:T(8,128)} %get-tuple-element.660), channel_id=1, source_target_pairs={{0,1},{1,2},{2,3},{3,4},{4,5},{5,6},{6,7},{7,0},{8,9},{9,10},{10,1... | collective-permute-start | bytes 6291464 | tf_op jit(solution)/shard_map/while/body/eval_jaxpr/ppermute | solution.py:75
  905.8 72.7 %collective-permute-start.5 = (f32[1,256,16,128]{3,1,2,0:T(8,128)}, f32[1,256,16,128]{3,1,2,0:T(8,128)}, u32[]{:S(2)}, u32[]{:S(2)}) collective-permute-start(f32[1,256,16,128]{3,1,2,0:T(8,128)} %get-tuple-element.661), channel_id=1, source_target_pairs={{0,1},{1,2},{2,3},{3,4},{4,5},{5,6},{6,7},{7,0},{8,9},{9,10},{10,1... | collective-permute-start | bytes 6291464 | tf_op jit(solution)/shard_map/while/body/eval_jaxpr/ppermute | solution.py:76
  905.8 59.2 %collective-permute-start.2 = (bf16[1,256,16,128]{3,1,2,0:T(8,128)(2,1)}, bf16[1,256,16,128]{3,1,2,0:T(8,128)(2,1)S(1)}, u32[]{:S(2)}, u32[]{:S(2)}) collective-permute-start(bf16[1,256,16,128]{3,1,2,0:T(8,128)(2,1)} %get-tuple-element.658), channel_id=1, source_target_pairs={{0,1},{1,2},{2,3},{3,4},{4,5},{5,6},{6,7},{7,0},{8,9},{9,10},{10,1... | collective-permute-start | bytes 3145736 | tf_op jit(solution)/shard_map/while/body/eval_jaxpr/ppermute | solution.py:73
  905.8 70.4 %collective-permute-start.3 = (bf16[1,256,16,128]{3,1,2,0:T(8,128)(2,1)}, bf16[1,256,16,128]{3,1,2,0:T(8,128)(2,1)}, u32[]{:S(2)}, u32[]{:S(2)}) collective-permute-start(bf16[1,256,16,128]{3,1,2,0:T(8,128)(2,1)} %get-tuple-element.659), channel_id=1, source_target_pairs={{0,1},{1,2},{2,3},{3,4},{4,5},{5,6},{6,7},{7,0},{8,9},{9,10},{10,1... | collective-permute-start | bytes 3145736 | tf_op jit(solution)/shard_map/while/body/eval_jaxpr/ppermute | solution.py:74
  988.0 14.3 %collective-permute-start.6 = (bf16[1,256,16,128]{3,2,1,0:T(8,128)(2,1)S(1)}, bf16[1,256,16,128]{3,2,1,0:T(8,128)(2,1)S(1)}, u32[]{:S(2)}, u32[]{:S(2)}) collective-permute-start(bf16[1,256,16,128]{3,2,1,0:T(8,128)(2,1)S(1)} %copy.29), channel_id=1, source_target_pairs={{0,1},{1,2},{2,3},{3,4},{4,5},{5,6},{6,7},{7,0},{8,9},{9,10},{10,1... | collective-permute-start | bytes 3145736 | tf_op jit(solution)/shard_map/ppermute | solution.py:87
  989.3 24.2 %collective-permute-start.7 = (bf16[1,256,16,128]{3,2,1,0:T(8,128)(2,1)S(1)}, bf16[1,256,16,128]{3,2,1,0:T(8,128)(2,1)}, u32[]{:S(2)}, u32[]{:S(2)}) collective-permute-start(bf16[1,256,16,128]{3,2,1,0:T(8,128)(2,1)S(1)} %copy.30), channel_id=1, source_target_pairs={{0,1},{1,2},{2,3},{3,4},{4,5},{5,6},{6,7},{7,0},{8,9},{9,10},{10,1... | collective-permute-start | bytes 3145736 | tf_op jit(solution)/shard_map/ppermute | solution.py:88
  990.0 6.1 copy-start.5
  (22 other events, 46.4 us)
where the time goes:
time: 1030 us; the launch traced here: 1020 us
  waiting for transfers between devices  677 us (66%)
  matrix products  177 us (17%)
  local copies, waits for them, and re-layouts  133 us (13%)
  other arithmetic  27.2 us (3%)
    ppermute x7, waiting for transfers between devices, backward_body(): key_cur = lax.ppermute(key_cur, 'cp', shift_pairs)  413 us
    ppermute x7, waiting for transfers between devices, forward_body(): key_cur = lax.ppermute(key_cur, 'cp', shift_pairs)  99.3 us
    while x42, local copies, waits for them, and re-layouts  89.9 us
    ppermute x7, waiting for transfers between devices, forward_body(): value_cur = lax.ppermute(value_cur, 'cp', shift_pairs)  78.6 us
    ppermute x7, waiting for transfers between devices, backward_body(): value_cur = lax.ppermute(value_cur, 'cp', shift_pairs)  71.4 us
    dot_general x7, matrix products, backward_step(): jnp.einsum('bgrqk,bqgrd->bkgd', grad_score, query5, preferred_element_typ...  37.2 us
    dot_general x7, matrix products, backward_step(): jnp.einsum('bgrqk,bqgrd->bkgd', prob_low, grad5, preferred_element_type=j...  35.7 us
    dot_general x7, matrix products, forward_step(): jnp.einsum('bgrqk,bkgd->bgrqd', weights.astype(jnp.bfloat16), value_blk,...  29.1 us
  transfers between devices with their start and end apart: 44, of which 30 were waited for; matrix products, arithmetic and copies ran while one was open for 3% of the time, Pallas kernels for 0%

commit v1 on v0

v1 whole, which is shorter than its diff:
```python
import functools

import jax
import jax.numpy as jnp
from jax import lax
from jax.experimental import pallas as pl
from jax.experimental.pallas import tpu as pltpu
from jax.sharding import PartitionSpec as P

MESH = pl.DeviceIdType.MESH
F32 = jnp.float32
BF16 = jnp.bfloat16
NT = (((1,), (1,)), ((), ()))


def attention_kernel(n, groups, ratio, tokens, dim, q_in, k_in, v_in, g_in, o_out, dq_out, dk_out, dv_out, lse_out, qb, kb, vb, gb, ob, dqb, dkb, dvb, lseb, s_scr, dk_acc, dv_acc, kt, vt, t_scr, in_send, in_recv, out_send, out_recv, lse_send, lse_recv, in_local, out_local, lse_local):
    me = lax.axis_index("cp")
    scale = dim ** -0.5
    wide = ratio * dim

    def peer(offset):
        return {"cp": lax.rem(me + offset, n)}

    def row_of(device):
        return pl.ds(pl.multiple_of(device * tokens, tokens), tokens)

    def column_of(head, width):
        return pl.ds(pl.multiple_of(head * width, width), width)

    barrier = pltpu.get_barrier_semaphore()
    for offset in range(1, n):
        pl.semaphore_signal(barrier, inc=1, device_id=peer(offset), device_id_type=MESH)
    pl.semaphore_wait(barrier, n - 1)

    in_arrays = ((k_in, kb, dim), (v_in, vb, dim), (q_in, qb, wide), (g_in, gb, wide))
    in_copies = {}
    for g in range(groups):
        for offset in range(1, n):
            target = lax.rem(me + offset, n)
            for a, (src, dst, width) in enumerate(in_arrays):
                copy = pltpu.make_async_remote_copy(
                    src_ref=src.at[:, column_of(target * groups + g, width)],
                    dst_ref=dst.at[g, row_of(me)],
                    send_sem=in_send.at[g, offset - 1, a],
                    recv_sem=in_recv.at[g, offset - 1, a],
                    device_id=peer(offset),
                    device_id_type=MESH,
                )
                copy.start()
                in_copies[g, offset, a] = copy
        for a, (src, dst, width) in enumerate(in_arrays):
            copy = pltpu.make_async_copy(src.at[:, column_of(me * groups + g, width)], dst.at[g, row_of(me)], in_local.at[g, a])
            copy.start()
            in_copies[g, 0, a] = copy

    key_pos = lax.broadcasted_iota(jnp.int32, (tokens, tokens), 0)
    query_pos = lax.broadcasted_iota(jnp.int32, (tokens, tokens), 1)

    def fold(x, op):
        return op(x.reshape(tokens // 8, 8, tokens), axis=0)

    def head_compute(g):
        def prepare(j, _):
            rows = row_of(j)
            kt[:, rows] = jnp.transpose(kb[g, rows, :].astype(F32)).astype(BF16)
            vt[:, rows] = jnp.transpose(vb[g, rows, :].astype(F32)).astype(BF16)
            dk_acc[rows, :] = jnp.zeros((tokens, dim), F32)
            dv_acc[rows, :] = jnp.zeros((tokens, dim), F32)
            return 0

        lax.fori_loop(0, n, prepare, 0)

        def block(i, _):
            rows_i = row_of(i)
            qs = [qb[g, rows_i, r * dim:(r + 1) * dim] for r in range(ratio)]
            gs = [gb[g, rows_i, r * dim:(r + 1) * dim] for r in range(ratio)]

            def score(j, maxes):
                rows = row_of(j)
                key_blk = kb[g, rows, :]
                new = []
                for r in range(ratio):
                    s = lax.dot_general(key_blk, qs[r], NT, preferred_element_type=F32)
                    s_scr[r, rows, :] = s
                    new.append(jnp.maximum(maxes[r], fold(s, jnp.max)))
                return tuple(new)

            maxes = lax.fori_loop(0, i, score, tuple(jnp.full((8, tokens), -jnp.inf, F32) for _ in range(ratio)))
            key_blk = kb[g, rows_i, :]
            tops = []
            for r in range(ratio):
                s = lax.dot_general(key_blk, qs[r], NT, preferred_element_type=F32)
                s = jnp.where(key_pos <= query_pos, s, -jnp.inf)
                s_scr[r, rows_i, :] = s
                tops.append(jnp.max(jnp.maximum(maxes[r], fold(s, jnp.max)), axis=0, keepdims=True))

            def weigh(j, sums):
                rows = row_of(j)
                new = []
                for r in range(ratio):
                    p = jnp.exp((s_scr[r, rows, :] - tops[r]) * scale)
                    s_scr[r, rows, :] = p
                    new.append(sums[r] + fold(p, jnp.sum))
                return tuple(new)

            sums = lax.fori_loop(0, i + 1, weigh, tuple(jnp.zeros((8, tokens), F32) for _ in range(ratio)))
            totals = [jnp.sum(x, axis=0, keepdims=True) for x in sums]
            invs = [1.0 / x for x in totals]
            for r in range(ratio):
                lseb[i, pl.ds(g * ratio + r, 1), :] = tops[r] * scale + jnp.log(totals[r])
                t_scr[r] = jnp.zeros((dim, tokens), F32)

            def outputs(j, _):
                rows = row_of(j)
                vt_blk = vt[:, rows]
                dv_new = dv_acc[rows, :]
                for r in range(ratio):
                    p_low = (s_scr[r, rows, :] * invs[r]).astype(BF16)
                    t_scr[r] += jnp.dot(vt_blk, p_low, preferred_element_type=F32)
                    dv_new += jnp.dot(p_low, gs[r], preferred_element_type=F32)
                dv_acc[rows, :] = dv_new
                return 0

            lax.fori_loop(0, i + 1, outputs, 0)
            deltas = []
            for r in range(ratio):
                out = jnp.transpose(t_scr[r]).astype(BF16)
                ob[g, rows_i, r * dim:(r + 1) * dim] = out
                deltas.append(jnp.sum(jnp.transpose(gs[r].astype(F32) * out.astype(F32)), axis=0, keepdims=True))
            for r in range(ratio):
                t_scr[r] = jnp.zeros((dim, tokens), F32)

            def gradients(j, _):
                rows = row_of(j)
                kt_blk = kt[:, rows]
                value_blk = vb[g, rows, :]
                dk_new = dk_acc[rows, :]
                for r in range(ratio):
                    dp = lax.dot_general(value_blk, gs[r], NT, preferred_element_type=F32)
                    ds = ((s_scr[r, rows, :] * invs[r]) * (dp - deltas[r])).astype(BF16)
                    t_scr[r] += jnp.dot(kt_blk, ds, preferred_element_type=F32)
                    dk_new += jnp.dot(ds, qs[r], preferred_element_type=F32)
                dk_acc[rows, :] = dk_new
                return 0

            lax.fori_loop(0, i + 1, gradients, 0)
            for r in range(ratio):
                dqb[g, rows_i, r * dim:(r + 1) * dim] = jnp.transpose(t_scr[r] * scale).astype(BF16)
            return 0

        lax.fori_loop(0, n, block, 0)

        def finish(j, _):
            rows = row_of(j)
            dkb[g, rows, :] = (dk_acc[rows, :] * scale).astype(BF16)
            dvb[g, rows, :] = dv_acc[rows, :].astype(BF16)
            return 0

        lax.fori_loop(0, n, finish, 0)

    out_arrays = ((ob, o_out, wide), (dqb, dq_out, wide), (dkb, dk_out, dim), (dvb, dv_out, dim))
    out_copies = {}
    for g in range(groups):
        for offset in range(n):
            for a in range(4):
                if offset:
                    in_copies[g, offset, a].wait_recv()
                else:
                    in_copies[g, offset, a].wait()
        head_compute(g)
        for offset in range(1, n):
            target = lax.rem(me + offset, n)
            for a, (src, dst, width) in enumerate(out_arrays):
                copy = pltpu.make_async_remote_copy(
                    src_ref=src.at[g, row_of(target)],
                    dst_ref=dst.at[:, column_of(me * groups + g, width)],
                    send_sem=out_send.at[g, offset - 1, a],
                    recv_sem=out_recv.at[g, offset - 1, a],
                    device_id=peer(offset),
                    device_id_type=MESH,
                )
                copy.start()
                out_copies[g, offset, a] = copy
        for a, (src, dst, width) in enumerate(out_arrays):
            copy = pltpu.make_async_copy(src.at[g, row_of(me)], dst.at[:, column_of(me * groups + g, width)], out_local.at[g, a])
            copy.start()
            out_copies[g, 0, a] = copy

    lse_copies = []
    for offset in range(1, n):
        target = lax.rem(me + offset, n)
        copy = pltpu.make_async_remote_copy(
            src_ref=lseb.at[target],
            dst_ref=lse_out.at[me],
            send_sem=lse_send.at[offset - 1],
            recv_sem=lse_recv.at[offset - 1],
            device_id=peer(offset),
            device_id_type=MESH,
        )
        copy.start()
        lse_copies.append(copy)
    copy = pltpu.make_async_copy(lseb.at[me], lse_out.at[me], lse_local)
    copy.start()
    lse_copies.append(copy)

    for (g, offset, a), copy in in_copies.items():
        if offset:
            copy.wait_send()
    for copy in out_copies.values():
        copy.wait()
    for copy in lse_copies:
        copy.wait()


def solution(mesh):
    n = mesh.shape["cp"]

    def attention_shard(queries, keys, values, out_grad):
        batch, tokens, heads, dim = queries.shape
        kv_heads = keys.shape[2]
        ratio = heads // kv_heads
        groups = kv_heads // n
        total = n * tokens
        wide = ratio * dim
        stats = -(-groups * ratio // 8) * 8

        def flat(x):
            return x.reshape(tokens, x.shape[2] * dim)

        any_space = pl.BlockSpec(memory_space=pl.ANY)
        dma = pltpu.SemaphoreType.DMA
        out, dq, dk, dv, lse = pl.pallas_call(
            functools.partial(attention_kernel, n, groups, ratio, tokens, dim),
            out_shape=(
                jax.ShapeDtypeStruct((tokens, heads * dim), BF16),
                jax.ShapeDtypeStruct((tokens, heads * dim), BF16),
                jax.ShapeDtypeStruct((tokens, kv_heads * dim), BF16),
                jax.ShapeDtypeStruct((tokens, kv_heads * dim), BF16),
                jax.ShapeDtypeStruct((n, stats, tokens), F32),
            ),
            in_specs=[any_space] * 4,
            out_specs=(any_space,) * 5,
            scratch_shapes=[
                pltpu.VMEM((groups, total, wide), BF16),
                pltpu.VMEM((groups, total, dim), BF16),
                pltpu.VMEM((groups, total, dim), BF16),
                pltpu.VMEM((groups, total, wide), BF16),
                pltpu.VMEM((groups, total, wide), BF16),
                pltpu.VMEM((groups, total, wide), BF16),
                pltpu.VMEM((groups, total, dim), BF16),
                pltpu.VMEM((groups, total, dim), BF16),
                pltpu.VMEM((n, stats, tokens), F32),
                pltpu.VMEM((ratio, total, tokens), F32),
                pltpu.VMEM((total, dim), F32),
                pltpu.VMEM((total, dim), F32),
                pltpu.VMEM((dim, total), BF16),
                pltpu.VMEM((dim, total), BF16),
                pltpu.VMEM((ratio, dim, tokens), F32),
                dma((groups, n - 1, 4)),
                dma((groups, n - 1, 4)),
                dma((groups, n - 1, 4)),
                dma((groups, n - 1, 4)),
                dma((n - 1,)),
                dma((n - 1,)),
                dma((groups, 4)),
                dma((groups, 4)),
                dma,
            ],
            compiler_params=pltpu.CompilerParams(collective_id=0, has_side_effects=True, vmem_limit_bytes=60 * 2**20),
            name="heads_attention",
        )(flat(queries), flat(keys), flat(values), flat(out_grad))
        shape = (batch, tokens, heads, dim)
        kv_shape = (batch, tokens, kv_heads, dim)
        row_lse = lse[:, :groups * ratio, :].reshape(batch, heads, tokens)
        return out.reshape(shape), row_lse, dq.reshape(shape), dk.reshape(kv_shape), dv.reshape(kv_shape)

    seq_spec = P("dp", "cp")
    return jax.shard_map(attention_shard, mesh=mesh, in_specs=(seq_spec,) * 4, out_specs=(seq_spec, P("dp", None, "cp"), seq_spec, seq_spec, seq_spec), check_vma=False)
```

time: 1030 us -> 178 us (0.17)
  the two profiles are of different devices: /device:TPU:94 before, /device:TPU:81 now
where the time goes in v1:
time: 178 us; the launch traced here: 177 us
  Pallas kernels  159 us (89%)
  local copies, waits for them, and re-layouts  18 us (10%)
    pallas_call x1, Pallas kernels, attention_shard(): pl.pallas_call(functools.partial(attention_kernel, n, groups, ratio, toke...  159 us
    reshape x2, local copies, waits for them, and re-layouts, flat(): return x.reshape(tokens, x.shape[2] * dim)  9.64 us
    unnamed x16, local copies, waits for them, and re-layouts  7.72 us

profile of v1, /device:TPU:81, one launch (start us, length us, event | category | flops | bytes accessed | tf_op | source)
XLA Modules:
  0.0 177.4 jit_solution(349914862343275562)
XLA Ops:
  0.6 0.0 copy-start.1
  0.6 0.0 copy-start.2
  0.7 3.5 %copy_bitcast_fusion.2 = (bf16[256,2048]{1,0:T(8,128)(2,1)}, bf16[256,2048]{1,0:T(8,128)(2,1)}) fusion(bf16[32,8,16,128]{3,2,1,0:T(8,128)(2,1)} %bitcast.38, bf16[32,8,16,128]{3,2,1,0:T(8,128)(2,1)} %bitcast.39), kind=kLoop, calls=%fused_computation.2 | loop fusion | bytes 4194304 | tf_op jit(solution)/shard_map/reshape | solution.py:228
  4.2 0.0 copy-done.1
  4.2 0.0 copy-done.2
  4.2 6.1 %copy_bitcast_fusion = (bf16[256,4096]{1,0:T(8,128)(2,1)}, bf16[256,4096]{1,0:T(8,128)(2,1)}) fusion(bf16[32,8,32,128]{3,2,1,0:T(8,128)(2,1)S(1)} %bitcast.32, bf16[32,8,32,128]{3,2,1,0:T(8,128)(2,1)S(1)} %bitcast.33), kind=kLoop, calls=%fused_computation | loop fusion | bytes 8388608 | tf_op jit(solution)/shard_map/reshape | solution.py:228
  10.3 158.7 %heads_attention.1 = (bf16[256,4096]{1,0:T(8,128)(2,1)}, bf16[256,4096]{1,0:T(8,128)(2,1)}, bf16[256,2048]{1,0:T(8,128)(2,1)}, bf16[256,2048]{1,0:T(8,128)(2,1)}, f32[8,8,256]{2,1,0:T(8,128)}) custom-call(bf16[256,4096]{1,0:T(8,128)(2,1)} %get-tuple-element.16.q_in, bf16[256,2048]{1,0:T(8,128)(2,1)} %get-tuple-element.18.k_in, ...), custom_call_target="tpu_custom_call" | custom-call | tf_op jit(solution)/shard_map/heads_attention/pallas_call | solution.py:232
  169.0 0.0 copy-start.5
  169.0 0.0 copy-start.4
  169.0 3.5 %copy.13 = bf16[32,8,32,128]{3,2,1,0:T(8,128)(2,1)} copy(bf16[32,8,32,128]{3,1,2,0:T(8,128)(2,1)} %bitcast.30) | data formatting | bytes 4194304
  172.5 0.0 copy-start.3
  172.5 0.0 copy-done.5
  172.5 0.6 reshape.42
  173.2 0.0 copy-done.4
  173.2 0.0 copy-start
  173.2 1.2 copy.15
  174.4 0.0 copy-done.3
  174.4 1.2 copy.16
  175.6 0.0 copy-done
  175.6 1.8 %copy.14 = bf16[32,8,32,128]{3,2,1,0:T(8,128)(2,1)} copy(bf16[32,8,32,128]{3,1,2,0:T(8,128)(2,1)S(1)} %bitcast.28) | data formatting | bytes 4194304
  (1 shorter events, 0.0 us)
Async XLA Ops:
  0.6 3.6 %copy-start.1 = (bf16[1,256,32,128]{3,2,1,0:T(8,128)(2,1)S(1)}, bf16[1,256,32,128]{3,2,1,0:T(8,128)(2,1)}, u32[]{:S(2)}) copy-start(bf16[1,256,32,128]{3,2,1,0:T(8,128)(2,1)} %param.7) | copy-start | bytes 6291460
  0.6 3.5 %copy-start.2 = (bf16[1,256,32,128]{3,2,1,0:T(8,128)(2,1)S(1)}, bf16[1,256,32,128]{3,2,1,0:T(8,128)(2,1)}, u32[]{:S(2)}) copy-start(bf16[1,256,32,128]{3,2,1,0:T(8,128)(2,1)} %param.4) | copy-start | bytes 6291460
  169.0 3.5 %copy-start.5 = (f32[8,8,256]{2,1,0:T(8,128)S(1)}, f32[8,8,256]{2,1,0:T(8,128)}, u32[]{:S(2)}) copy-start(f32[8,8,256]{2,1,0:T(8,128)} %get-tuple-element.11) | copy-start | bytes 196612
  169.0 4.1 %copy-start.4 = (bf16[256,2048]{1,0:T(8,128)(2,1)S(1)}, bf16[256,2048]{1,0:T(8,128)(2,1)}, u32[]{:S(2)}) copy-start(bf16[256,2048]{1,0:T(8,128)(2,1)} %get-tuple-element.13) | copy-start | bytes 3145732
  172.5 1.9 %copy-start.3 = (bf16[256,2048]{1,0:T(8,128)(2,1)S(1)}, bf16[256,2048]{1,0:T(8,128)(2,1)}, u32[]{:S(2)}) copy-start(bf16[256,2048]{1,0:T(8,128)(2,1)} %get-tuple-element.14) | copy-start | bytes 3145732
  173.2 2.4 %copy-start = (bf16[256,4096]{1,0:T(8,128)(2,1)S(1)}, bf16[256,4096]{1,0:T(8,128)(2,1)}, u32[]{:S(2)}) copy-start(bf16[256,4096]{1,0:T(8,128)(2,1)} %get-tuple-element.12) | copy-start | bytes 6291460

commit v2 on v1

--- a/solution.py
+++ b/solution.py
@@ -13,7 +13,7 @@
 NT = (((1,), (1,)), ((), ()))
 
 
-def attention_kernel(n, groups, ratio, tokens, dim, q_in, k_in, v_in, g_in, o_out, dq_out, dk_out, dv_out, lse_out, qb, kb, vb, gb, ob, dqb, dkb, dvb, lseb, s_scr, dk_acc, dv_acc, kt, vt, t_scr, in_send, in_recv, out_send, out_recv, lse_send, lse_recv, in_local, out_local, lse_local):
+def attention_kernel(n, groups, ratio, tokens, dim, q_in, k_in, v_in, g_in, o_out, dq_out, dk_out, dv_out, lse_out, qb, kb, vb, gb, ob, dqb, dkb, dvb, lseb, s_scr, dk_acc, dv_acc, kt, vt, t_scr, q_cat, g_cat, in_send, in_recv, out_send, out_recv, lse_send, lse_recv, in_local, out_local, lse_local):
     me = lax.axis_index("cp")
     scale = dim ** -0.5
     wide = ratio * dim
@@ -53,110 +53,100 @@
             copy.start()
             in_copies[g, 0, a] = copy
 
-    key_pos = lax.broadcasted_iota(jnp.int32, (tokens, tokens), 0)
-    query_pos = lax.broadcasted_iota(jnp.int32, (tokens, tokens), 1)
+    blk = q_cat.shape[0] // ratio
+    cols = ratio * blk
+    key_pos = lax.broadcasted_iota(jnp.int32, (blk, blk), 0)
+    query_pos = lax.broadcasted_iota(jnp.int32, (blk, blk), 1)
 
     def fold(x, op):
-        return op(x.reshape(tokens // 8, 8, tokens), axis=0)
+        return op(x.reshape(blk // 8, 8, cols), axis=0)
+
+    def block_of(index):
+        return pl.ds(pl.multiple_of(index * blk, blk), blk)
 
     def head_compute(g):
         def prepare(j, _):
-            rows = row_of(j)
+            rows = block_of(j)
             kt[:, rows] = jnp.transpose(kb[g, rows, :].astype(F32)).astype(BF16)
             vt[:, rows] = jnp.transpose(vb[g, rows, :].astype(F32)).astype(BF16)
-            dk_acc[rows, :] = jnp.zeros((tokens, dim), F32)
-            dv_acc[rows, :] = jnp.zeros((tokens, dim), F32)
+            dk_acc[rows, :] = jnp.zeros((blk, dim), F32)
+            dv_acc[rows, :] = jnp.zeros((blk, dim), F32)
             return 0
 
-        lax.fori_loop(0, n, prepare, 0)
+        lax.fori_loop(0, n * tokens // blk, prepare, 0)
 
         def block(i, _):
-            rows_i = row_of(i)
-            qs = [qb[g, rows_i, r * dim:(r + 1) * dim] for r in range(ratio)]
-            gs = [gb[g, rows_i, r * dim:(r + 1) * dim] for r in range(ratio)]
-
-            def score(j, maxes):
-                rows = row_of(j)
-                key_blk = kb[g, rows, :]
-                new = []
-                for r in range(ratio):
-                    s = lax.dot_general(key_blk, qs[r], NT, preferred_element_type=F32)
-                    s_scr[r, rows, :] = s
-                    new.append(jnp.maximum(maxes[r], fold(s, jnp.max)))
-                return tuple(new)
-
-            maxes = lax.fori_loop(0, i, score, tuple(jnp.full((8, tokens), -jnp.inf, F32) for _ in range(ratio)))
-            key_blk = kb[g, rows_i, :]
-            tops = []
-            for r in range(ratio):
-                s = lax.dot_general(key_blk, qs[r], NT, preferred_element_type=F32)
-                s = jnp.where(key_pos <= query_pos, s, -jnp.inf)
-                s_scr[r, rows_i, :] = s
-                tops.append(jnp.max(jnp.maximum(maxes[r], fold(s, jnp.max)), axis=0, keepdims=True))
-
-            def weigh(j, sums):
-                rows = row_of(j)
-                new = []
-                for r in range(ratio):
-                    p = jnp.exp((s_scr[r, rows, :] - tops[r]) * scale)
-                    s_scr[r, rows, :] = p
-                    new.append(sums[r] + fold(p, jnp.sum))
-                return tuple(new)
-
-            sums = lax.fori_loop(0, i + 1, weigh, tuple(jnp.zeros((8, tokens), F32) for _ in range(ratio)))
-            totals = [jnp.sum(x, axis=0, keepdims=True) for x in sums]
-            invs = [1.0 / x for x in totals]
-            for r in range(ratio):
-                lseb[i, pl.ds(g * ratio + r, 1), :] = tops[r] * scale + jnp.log(totals[r])
-                t_scr[r] = jnp.zeros((dim, tokens), F32)
+            rows_i = block_of(i)
+            for r in range(ratio):
+                q_cat[r * blk:(r + 1) * blk, :] = qb[g, rows_i, r * dim:(r + 1) * dim]
+                g_cat[r * blk:(r + 1) * blk, :] = gb[g, rows_i, r * dim:(r + 1) * dim]
+
+            def score(j, top):
+                rows = block_of(j)
+                s = lax.dot_general(kb[g, rows, :], q_cat[...], NT, preferred_element_type=F32)
+                s_scr[rows, :] = s
+                return jnp.maximum(top, fold(s, jnp.max))
+
+            top = lax.fori_loop(0, i, score, jnp.full((8, cols), -jnp.inf, F32))
+            s = lax.dot_general(kb[g, rows_i, :], q_cat[...], NT, preferred_element_type=F32)
+            keep = jnp.concatenate([key_pos <= query_pos] * ratio, axis=1)
+            s = jnp.where(keep, s, -jnp.inf)
+            s_scr[rows_i, :] = s
+            top = jnp.max(jnp.maximum(top, fold(s, jnp.max)), axis=0, keepdims=True)
+
+            def weigh(j, total):
+                rows = block_of(j)
+                p = jnp.exp((s_scr[rows, :] - top) * scale)
+                s_scr[rows, :] = p
+                return total + fold(p, jnp.sum)
+
+            total = lax.fori_loop(0, i + 1, weigh, jnp.zeros((8, cols), F32))
+            total = jnp.sum(total, axis=0, keepdims=True)
+            inv = 1.0 / total
+            lse = top * scale + jnp.log(total)
+            for r in range(ratio):
+                for t in range(blk // tokens):
+                    at = r * blk + t * tokens
+                    lseb[i * (blk // tokens) + t, pl.ds(g * ratio + r, 1), :] = lse[:, at:at + tokens]
+            t_scr[...] = jnp.zeros((dim, cols), F32)
 
             def outputs(j, _):
-                rows = row_of(j)
-                vt_blk = vt[:, rows]
-                dv_new = dv_acc[rows, :]
-                for r in range(ratio):
-                    p_low = (s_scr[r, rows, :] * invs[r]).astype(BF16)
-                    t_scr[r] += jnp.dot(vt_blk, p_low, preferred_element_type=F32)
-                    dv_new += jnp.dot(p_low, gs[r], preferred_element_type=F32)
-                dv_acc[rows, :] = dv_new
+                rows = block_of(j)
+                p_low = (s_scr[rows, :] * inv).astype(BF16)
+                t_scr[...] += jnp.dot(vt[:, rows], p_low, preferred_element_type=F32)
+                dv_acc[rows, :] += jnp.dot(p_low, g_cat[...], preferred_element_type=F32)
                 return 0
 
             lax.fori_loop(0, i + 1, outputs, 0)
-            deltas = []
-            for r in range(ratio):
-                out = jnp.transpose(t_scr[r]).astype(BF16)
-                ob[g, rows_i, r * dim:(r + 1) * dim] = out
-                deltas.append(jnp.sum(jnp.transpose(gs[r].astype(F32) * out.astype(F32)), axis=0, keepdims=True))
-            for r in range(ratio):
-                t_scr[r] = jnp.zeros((dim, tokens), F32)
+            out = jnp.transpose(t_scr[...]).astype(BF16)
+            for r in range(ratio):
+                ob[g, rows_i, r * dim:(r + 1) * dim] = out[r * blk:(r + 1) * blk]
+            delta = jnp.sum(jnp.transpose(g_cat[...].astype(F32) * out.astype(F32)), axis=0, keepdims=True)
+            t_scr[...] = jnp.zeros((dim, cols), F32)
 
             def gradients(j, _):
-                rows = row_of(j)
-                kt_blk = kt[:, rows]
-                value_blk = vb[g, rows, :]
-                dk_new = dk_acc[rows, :]
-                for r in range(ratio):
-                    dp = lax.dot_general(value_blk, gs[r], NT, preferred_element_type=F32)
-                    ds = ((s_scr[r, rows, :] * invs[r]) * (dp - deltas[r])).astype(BF16)
-                    t_scr[r] += jnp.dot(kt_blk, ds, preferred_element_type=F32)
-                    dk_new += jnp.dot(ds, qs[r], preferred_element_type=F32)
-                dk_acc[rows, :] = dk_new
+                rows = block_of(j)
+                dp = lax.dot_general(vb[g, rows, :], g_cat[...], NT, preferred_element_type=F32)
+                ds = ((s_scr[rows, :] * inv) * (dp - delta)).astype(BF16)
+                t_scr[...] += jnp.dot(kt[:, rows], ds, preferred_element_type=F32)
+                dk_acc[rows, :] += jnp.dot(ds, q_cat[...], preferred_element_type=F32)
                 return 0
 
             lax.fori_loop(0, i + 1, gradients, 0)
-            for r in range(ratio):
-                dqb[g, rows_i, r * dim:(r + 1) * dim] = jnp.transpose(t_scr[r] * scale).astype(BF16)
+            dq = jnp.transpose(t_scr[...] * scale).astype(BF16)
+            for r in range(ratio):
+                dqb[g, rows_i, r * dim:(r + 1) * dim] = dq[r * blk:(r + 1) * blk]
             return 0
 
-        lax.fori_loop(0, n, block, 0)
+        lax.fori_loop(0, n * tokens // blk, block, 0)
 
         def finish(j, _):
-            rows = row_of(j)
+            rows = block_of(j)
             dkb[g, rows, :] = (dk_acc[rows, :] * scale).astype(BF16)
             dvb[g, rows, :] = dv_acc[rows, :].astype(BF16)
             return 0
 
-        lax.fori_loop(0, n, finish, 0)
+        lax.fori_loop(0, n * tokens // blk, finish, 0)
 
     out_arrays = ((ob, o_out, wide), (dqb, dq_out, wide), (dkb, dk_out, dim), (dvb, dv_out, dim))
     out_copies = {}
@@ -222,6 +212,7 @@
         groups = kv_heads // n
         total = n * tokens
         wide = ratio * dim
+        blk = 2 * tokens
         stats = -(-groups * ratio // 8) * 8
 
         def flat(x):
@@ -250,12 +241,14 @@
                 pltpu.VMEM((groups, total, dim), BF16),
                 pltpu.VMEM((groups, total, dim), BF16),
                 pltpu.VMEM((n, stats, tokens), F32),
-                pltpu.VMEM((ratio, total, tokens), F32),
+                pltpu.VMEM((total, ratio * blk), F32),
                 pltpu.VMEM((total, dim), F32),
                 pltpu.VMEM((total, dim), F32),
                 pltpu.VMEM((dim, total), BF16),
                 pltpu.VMEM((dim, total), BF16),
-                pltpu.VMEM((ratio, dim, tokens), F32),
+                pltpu.VMEM((dim, ratio * blk), F32),
+                pltpu.VMEM((ratio * blk, dim), BF16),
+                pltpu.VMEM((ratio * blk, dim), BF16),
                 dma((groups, n - 1, 4)),
                 dma((groups, n - 1, 4)),
                 dma((groups, n - 1, 4)),

time: 178 us -> 164 us (0.921)
  Pallas kernels: 159 us -> 145 us
    pallas_call x1, Pallas kernels: 159 us -> 145 us  [attention_shard(): pl.pallas_call(functools.partial(attention_kernel, n, groups, ratio, toke...]
where the time goes in v2:
time: 164 us; the launch traced here: 163 us
  Pallas kernels  145 us (88%)
  local copies, waits for them, and re-layouts  18 us (11%)
    pallas_call x1, Pallas kernels, attention_shard(): pl.pallas_call(functools.partial(attention_kernel, n, groups, ratio, toke...  145 us
    reshape x2, local copies, waits for them, and re-layouts, flat(): return x.reshape(tokens, x.shape[2] * dim)  9.64 us
    unnamed x16, local copies, waits for them, and re-layouts  7.72 us

profile of v2, /device:TPU:81, one launch (start us, length us, event | category | flops | bytes accessed | tf_op | source)
XLA Modules:
  0.0 163.5 jit_solution(9297182186053441174)
XLA Ops:
  0.6 0.0 copy-start.1
  0.6 0.0 copy-start.2
  0.7 3.5 %copy_bitcast_fusion.2 = (bf16[256,2048]{1,0:T(8,128)(2,1)}, bf16[256,2048]{1,0:T(8,128)(2,1)}) fusion(bf16[32,8,16,128]{3,2,1,0:T(8,128)(2,1)} %bitcast.38, bf16[32,8,16,128]{3,2,1,0:T(8,128)(2,1)} %bitcast.39), kind=kLoop, calls=%fused_computation.2 | loop fusion | bytes 4194304 | tf_op jit(solution)/shard_map/reshape | solution.py:219
  4.2 0.0 copy-done.1
  4.2 0.0 copy-done.2
  4.2 6.1 %copy_bitcast_fusion = (bf16[256,4096]{1,0:T(8,128)(2,1)}, bf16[256,4096]{1,0:T(8,128)(2,1)}) fusion(bf16[32,8,32,128]{3,2,1,0:T(8,128)(2,1)S(1)} %bitcast.32, bf16[32,8,32,128]{3,2,1,0:T(8,128)(2,1)S(1)} %bitcast.33), kind=kLoop, calls=%fused_computation | loop fusion | bytes 8388608 | tf_op jit(solution)/shard_map/reshape | solution.py:219
  10.3 144.8 %heads_attention.1 = (bf16[256,4096]{1,0:T(8,128)(2,1)}, bf16[256,4096]{1,0:T(8,128)(2,1)}, bf16[256,2048]{1,0:T(8,128)(2,1)}, bf16[256,2048]{1,0:T(8,128)(2,1)}, f32[8,8,256]{2,1,0:T(8,128)}) custom-call(bf16[256,4096]{1,0:T(8,128)(2,1)} %get-tuple-element.16.q_in, bf16[256,2048]{1,0:T(8,128)(2,1)} %get-tuple-element.18.k_in, ...), custom_call_target="tpu_custom_call" | custom-call | tf_op jit(solution)/shard_map/heads_attention/pallas_call | solution.py:223
  155.1 0.0 copy-start.5
  155.1 0.0 copy-start.4
  155.1 3.5 %copy.13 = bf16[32,8,32,128]{3,2,1,0:T(8,128)(2,1)} copy(bf16[32,8,32,128]{3,1,2,0:T(8,128)(2,1)} %bitcast.30) | data formatting | bytes 4194304
  158.6 0.0 copy-start.3
  158.6 0.0 copy-done.5
  158.6 0.6 reshape.42
  159.2 0.0 copy-done.4
  159.2 0.0 copy-start
  159.2 1.2 copy.15
  160.4 0.0 copy-done.3
  160.4 1.2 copy.16
  161.7 0.0 copy-done
  161.7 1.8 %copy.14 = bf16[32,8,32,128]{3,2,1,0:T(8,128)(2,1)} copy(bf16[32,8,32,128]{3,1,2,0:T(8,128)(2,1)S(1)} %bitcast.28) | data formatting | bytes 4194304
  (1 shorter events, 0.0 us)
Async XLA Ops:
  0.6 3.6 %copy-start.1 = (bf16[1,256,32,128]{3,2,1,0:T(8,128)(2,1)S(1)}, bf16[1,256,32,128]{3,2,1,0:T(8,128)(2,1)}, u32[]{:S(2)}) copy-start(bf16[1,256,32,128]{3,2,1,0:T(8,128)(2,1)} %param.7) | copy-start | bytes 6291460
  0.6 3.5 %copy-start.2 = (bf16[1,256,32,128]{3,2,1,0:T(8,128)(2,1)S(1)}, bf16[1,256,32,128]{3,2,1,0:T(8,128)(2,1)}, u32[]{:S(2)}) copy-start(bf16[1,256,32,128]{3,2,1,0:T(8,128)(2,1)} %param.4) | copy-start | bytes 6291460
  155.1 3.5 %copy-start.5 = (f32[8,8,256]{2,1,0:T(8,128)S(1)}, f32[8,8,256]{2,1,0:T(8,128)}, u32[]{:S(2)}) copy-start(f32[8,8,256]{2,1,0:T(8,128)} %get-tuple-element.11) | copy-start | bytes 196612
  155.1 4.1 %copy-start.4 = (bf16[256,2048]{1,0:T(8,128)(2,1)S(1)}, bf16[256,2048]{1,0:T(8,128)(2,1)}, u32[]{:S(2)}) copy-start(bf16[256,2048]{1,0:T(8,128)(2,1)} %get-tuple-element.13) | copy-start | bytes 3145732
  158.6 1.9 %copy-start.3 = (bf16[256,2048]{1,0:T(8,128)(2,1)S(1)}, bf16[256,2048]{1,0:T(8,128)(2,1)}, u32[]{:S(2)}) copy-start(bf16[256,2048]{1,0:T(8,128)(2,1)} %get-tuple-element.14) | copy-start | bytes 3145732
  159.2 2.4 %copy-start = (bf16[256,4096]{1,0:T(8,128)(2,1)S(1)}, bf16[256,4096]{1,0:T(8,128)(2,1)}, u32[]{:S(2)}) copy-start(bf16[256,4096]{1,0:T(8,128)(2,1)} %get-tuple-element.12) | copy-start | bytes 6291460

commit v3 on v2

--- a/solution.py
+++ b/solution.py
@@ -13,7 +13,7 @@
 NT = (((1,), (1,)), ((), ()))
 
 
-def attention_kernel(n, groups, ratio, tokens, dim, q_in, k_in, v_in, g_in, o_out, dq_out, dk_out, dv_out, lse_out, qb, kb, vb, gb, ob, dqb, dkb, dvb, lseb, s_scr, dk_acc, dv_acc, kt, vt, t_scr, q_cat, g_cat, in_send, in_recv, out_send, out_recv, lse_send, lse_recv, in_local, out_local, lse_local):
+def attention_kernel(n, groups, ratio, tokens, dim, q_in, k_in, v_in, g_in, o_out, dq_out, dk_out, dv_out, lse_out, qb, kb, vb, gb, ob, dqb, dkb, dvb, lseb, s_scr, dk_acc, dv_acc, kt, vt, t_scr, q_cat, g_cat, q_stage, k_stage, v_stage, g_stage, q_send, k_send, v_send, g_send, f_scr, stage_sem, in_send, in_recv, out_send, out_recv, lse_send, lse_recv, in_local, out_local, lse_local):
     me = lax.axis_index("cp")
     scale = dim ** -0.5
     wide = ratio * dim
@@ -27,31 +27,76 @@
     def column_of(head, width):
         return pl.ds(pl.multiple_of(head * width, width), width)
 
+    stages = ((k_in, k_stage), (v_in, v_stage), (q_in, q_stage), (g_in, g_stage))
+    stage_copies = []
+    for a, (src, dst) in enumerate(stages):
+        copy = pltpu.make_async_copy(src, dst, stage_sem.at[a])
+        copy.start()
+        stage_copies.append(copy)
+
     barrier = pltpu.get_barrier_semaphore()
     for offset in range(1, n):
         pl.semaphore_signal(barrier, inc=1, device_id=peer(offset), device_id_type=MESH)
-    pl.semaphore_wait(barrier, n - 1)
-
-    in_arrays = ((k_in, kb, dim), (v_in, vb, dim), (q_in, qb, wide), (g_in, gb, wide))
+
+    def split_heads(stage, send):
+        heads = stage.shape[1]
+        per = heads // send.shape[0]
+        pad = heads + 8
+        step = 16
+
+        def widen(t, _):
+            base = t * step
+            part = stage[pl.ds(base, step)].astype(F32)
+            for u in range(step):
+                f_scr[pl.ds(pl.multiple_of((base + u) * pad, 8), heads), :] = part[u]
+            return 0
+
+        lax.fori_loop(0, tokens // step, widen, 0)
+
+        def gather(h, _):
+            for r in range(per):
+                send[h, :, r * dim:(r + 1) * dim] = f_scr[pl.ds(h * per + r, tokens, stride=pad), :].astype(BF16)
+            return 0
+
+        lax.fori_loop(0, send.shape[0], gather, 0)
+
+    in_arrays = ((k_send, kb), (v_send, vb), (q_send, qb), (g_send, gb))
     in_copies = {}
-    for g in range(groups):
+
+    def send_in(g, a):
+        src, dst = in_arrays[a]
         for offset in range(1, n):
             target = lax.rem(me + offset, n)
-            for a, (src, dst, width) in enumerate(in_arrays):
-                copy = pltpu.make_async_remote_copy(
-                    src_ref=src.at[:, column_of(target * groups + g, width)],
-                    dst_ref=dst.at[g, row_of(me)],
-                    send_sem=in_send.at[g, offset - 1, a],
-                    recv_sem=in_recv.at[g, offset - 1, a],
-                    device_id=peer(offset),
-                    device_id_type=MESH,
-                )
-                copy.start()
-                in_copies[g, offset, a] = copy
-        for a, (src, dst, width) in enumerate(in_arrays):
-            copy = pltpu.make_async_copy(src.at[:, column_of(me * groups + g, width)], dst.at[g, row_of(me)], in_local.at[g, a])
+            copy = pltpu.make_async_remote_copy(
+                src_ref=src.at[target * groups + g],
+                dst_ref=dst.at[g, row_of(me)],
+                send_sem=in_send.at[g, offset - 1, a],
+                recv_sem=in_recv.at[g, offset - 1, a],
+                device_id=peer(offset),
+                device_id_type=MESH,
+            )
             copy.start()
-            in_copies[g, 0, a] = copy
+            in_copies[g, offset, a] = copy
+        copy = pltpu.make_async_copy(src.at[me * groups + g], dst.at[g, row_of(me)], in_local.at[g, a])
+        copy.start()
+        in_copies[g, 0, a] = copy
+
+    stage_copies[0].wait()
+    split_heads(k_stage, k_send)
+    stage_copies[1].wait()
+    split_heads(v_stage, v_send)
+    pl.semaphore_wait(barrier, n - 1)
+    send_in(0, 0)
+    stage_copies[2].wait()
+    split_heads(q_stage, q_send)
+    send_in(0, 1)
+    stage_copies[3].wait()
+    split_heads(g_stage, g_send)
+    send_in(0, 2)
+    send_in(0, 3)
+    for g in range(1, groups):
+        for a in range(4):
+            send_in(g, a)
 
     blk = q_cat.shape[0] // ratio
     cols = ratio * blk
@@ -216,7 +261,7 @@
         stats = -(-groups * ratio // 8) * 8
 
         def flat(x):
-            return x.reshape(tokens, x.shape[2] * dim)
+            return x.reshape(tokens, x.shape[2], dim)
 
         any_space = pl.BlockSpec(memory_space=pl.ANY)
         dma = pltpu.SemaphoreType.DMA
@@ -249,6 +294,16 @@
                 pltpu.VMEM((dim, ratio * blk), F32),
                 pltpu.VMEM((ratio * blk, dim), BF16),
                 pltpu.VMEM((ratio * blk, dim), BF16),
+                pltpu.VMEM((tokens, heads, dim), BF16),
+                pltpu.VMEM((tokens, kv_heads, dim), BF16),
+                pltpu.VMEM((tokens, kv_heads, dim), BF16),
+                pltpu.VMEM((tokens, heads, dim), BF16),
+                pltpu.VMEM((kv_heads, tokens, wide), BF16),
+                pltpu.VMEM((kv_heads, tokens, dim), BF16),
+                pltpu.VMEM((kv_heads, tokens, dim), BF16),
+                pltpu.VMEM((kv_heads, tokens, wide), BF16),
+                pltpu.VMEM((tokens * (heads + 8), dim), F32),
+                dma((4,)),
                 dma((groups, n - 1, 4)),
                 dma((groups, n - 1, 4)),
                 dma((groups, n - 1, 4)),

time: 164 us -> 155 us (0.945)
  local copies, waits for them, and re-layouts: 18 us -> 8.35 us
    reshape x2 -> x0, local copies, waits for them, and re-layouts: 9.64 us -> none  [flat(): return x.reshape(tokens, x.shape[2] * dim)]
    unnamed x16 -> x12, local copies, waits for them, and re-layouts: 7.72 us -> 7.72 us
where the time goes in v3:
time: 155 us
  Pallas kernels  146 us (94%)
  local copies, waits for them, and re-layouts  8.35 us (5%)
    pallas_call x1, Pallas kernels, attention_shard(): pl.pallas_call(functools.partial(attention_kernel, n, groups, ratio, toke...  146 us
    unnamed x12, local copies, waits for them, and re-layouts  7.72 us

profile of v3, /device:TPU:81, one launch (start us, length us, event | category | flops | bytes accessed | tf_op | source)
XLA Modules:
  0.0 155.1 jit_solution(8662966412323928733)
XLA Ops:
  0.6 146.1 %heads_attention.1 = (bf16[256,4096]{1,0:T(8,128)(2,1)}, bf16[256,4096]{1,0:T(8,128)(2,1)}, bf16[256,2048]{1,0:T(8,128)(2,1)}, bf16[256,2048]{1,0:T(8,128)(2,1)}, f32[8,8,256]{2,1,0:T(8,128)}) custom-call(bf16[256,32,128]{2,1,0:T(8,128)(2,1)} %bitcast.16, bf16[256,16,128]{2,1,0:T(8,128)(2,1)} %bitcast.26, bf16[256,16,128]{2,1,0:T(8,128)(2,1)} %bitcast.27, ...), custom_call_target="tpu_custom_call" | custom-call | tf_op jit(solution)/shard_map/heads_attention/pallas_call | solution.py:268
  146.8 0.0 copy-start.3
  146.8 0.0 copy-start.2
  146.8 3.5 %copy.9 = bf16[32,8,32,128]{3,2,1,0:T(8,128)(2,1)} copy(bf16[32,8,32,128]{3,1,2,0:T(8,128)(2,1)} %bitcast.21) | data formatting | bytes 4194304
  150.3 0.0 copy-start.1
  150.3 0.0 copy-done.3
  150.3 0.6 reshape.42
  150.9 0.0 copy-done.2
  150.9 0.0 copy-start
  150.9 1.2 copy.11
  152.1 0.0 copy-done.1
  152.1 1.2 copy.12
  153.3 0.0 copy-done
  153.3 1.8 %copy.10 = bf16[32,8,32,128]{3,2,1,0:T(8,128)(2,1)} copy(bf16[32,8,32,128]{3,1,2,0:T(8,128)(2,1)S(1)} %bitcast.19) | data formatting | bytes 4194304
  (1 shorter events, 0.0 us)
Async XLA Ops:
  146.8 3.5 %copy-start.3 = (f32[8,8,256]{2,1,0:T(8,128)S(1)}, f32[8,8,256]{2,1,0:T(8,128)}, u32[]{:S(2)}) copy-start(f32[8,8,256]{2,1,0:T(8,128)} %get-tuple-element.11) | copy-start | bytes 196612
  146.8 4.1 %copy-start.2 = (bf16[256,2048]{1,0:T(8,128)(2,1)S(1)}, bf16[256,2048]{1,0:T(8,128)(2,1)}, u32[]{:S(2)}) copy-start(bf16[256,2048]{1,0:T(8,128)(2,1)} %get-tuple-element.13) | copy-start | bytes 3145732
  150.3 1.9 %copy-start.1 = (bf16[256,2048]{1,0:T(8,128)(2,1)S(1)}, bf16[256,2048]{1,0:T(8,128)(2,1)}, u32[]{:S(2)}) copy-start(bf16[256,2048]{1,0:T(8,128)(2,1)} %get-tuple-element.14) | copy-start | bytes 3145732
  150.9 2.4 %copy-start = (bf16[256,4096]{1,0:T(8,128)(2,1)S(1)}, bf16[256,4096]{1,0:T(8,128)(2,1)}, u32[]{:S(2)}) copy-start(bf16[256,4096]{1,0:T(8,128)(2,1)} %get-tuple-element.12) | copy-start | bytes 6291460

commit v4 on v2

v4 whole, which is shorter than its diff:
```python
import functools

import jax
import jax.numpy as jnp
from jax import lax
from jax.experimental import pallas as pl
from jax.experimental.pallas import tpu as pltpu
from jax.sharding import PartitionSpec as P

MESH = pl.DeviceIdType.MESH
F32 = jnp.float32
BF16 = jnp.bfloat16
NT = (((1,), (1,)), ((), ()))
CORES = 2
JOB_CHIPS = 2


def attention_kernel(n, groups, ratio, tokens, dim, q_in, k_in, v_in, g_in, o_out, dq_out, dk_out, dv_out, lse_out, qb, kb, vb, gb, ob, dqb, dkb, dvb, lseb, s_scr, dk_acc, dv_acc, kt, vt, t_scr, q_cat, g_cat, q_stage, k_stage, v_stage, g_stage, q_send, k_send, v_send, g_send, f_scr, jq, jk, jv, jg, jl, j_own, j_part, j_recv, o_part, stage_sem, in_send, in_recv, out_send, out_recv, lse_send, lse_recv, in_local, out_local, lse_local, ji_send, ji_recv, ji_local, jk_send, jk_recv, jo_send, jo_recv, jo_local, jl_send, jl_recv, jl_local, o_part_send, j_part_send, part_recv, fin_send, fin_recv, fin_local):
    me = lax.axis_index("cp")
    chip = lax.div(me, CORES)
    core = lax.rem(me, CORES)
    chips = n // CORES
    scale = dim ** -0.5
    wide = ratio * dim
    blk = CORES * tokens
    cols = ratio * blk
    rows_total = chips * blk
    slots = (chips - 1) * groups
    jobs = jnp.where(chip == 0, slots, jnp.where(chip == 1, groups, 0))

    def first_row(owner_chip):
        return lax.div(owner_chip + 1, 2)

    def peer(offset):
        return {"cp": lax.rem(me + offset, n)}

    partner = {"cp": me + 1 - 2 * core}

    def row_of(device):
        return pl.ds(pl.multiple_of(device * tokens, tokens), tokens)

    def block_of(index):
        return pl.ds(pl.multiple_of(index * blk, blk), blk)

    def column_of(head, width):
        return pl.ds(pl.multiple_of(head * width, width), width)

    def remote(src, dst, send_sem, recv_sem, device):
        return pltpu.make_async_remote_copy(src_ref=src, dst_ref=dst, send_sem=send_sem, recv_sem=recv_sem, device_id=device, device_id_type=MESH)

    pending = []

    def launch(copy, sends=None, receives=None):
        if sends is None:
            copy.start()
        else:
            pl.when(sends)(copy.start)
        pending.append((copy.wait_send, sends))
        return (copy, receives)

    def landed(entry):
        copy, receives = entry
        if receives is None:
            copy.wait_recv()
        else:
            pl.when(receives)(copy.wait_recv)

    def local(src, dst, sem, cond=None):
        copy = pltpu.make_async_copy(src, dst, sem)
        if cond is None:
            copy.start()
        else:
            pl.when(cond)(copy.start)
        return (copy, cond)

    def done(entry):
        copy, cond = entry
        if cond is None:
            copy.wait()
        else:
            pl.when(cond)(copy.wait)

    stage_copies = [local(src, dst, stage_sem.at[a]) for a, (src, dst) in enumerate(((k_in, k_stage), (v_in, v_stage), (q_in, q_stage), (g_in, g_stage)))]

    barrier = pltpu.get_barrier_semaphore()
    for offset in range(1, n):
        pl.semaphore_signal(barrier, inc=1, device_id=peer(offset), device_id_type=MESH)

    def split_heads(stage, send):
        heads = stage.shape[1]
        per = heads // send.shape[0]
        pad = heads + 8
        step = 16
        half = tokens // 2
        for part in range(2):
            def widen(t, _):
                base = t * step
                piece = stage[pl.ds(part * half + base, step)].astype(F32)
                for u in range(step):
                    f_scr[pl.ds(pl.multiple_of((base + u) * pad, 8), heads), :] = piece[u]
                return 0

            lax.fori_loop(0, half // step, widen, 0)

            def gather(h, _):
                for r in range(per):
                    send[h, part * half:(part + 1) * half, r * dim:(r + 1) * dim] = f_scr[pl.ds(h * per + r, half, stride=pad), :].astype(BF16)
                return 0

            lax.fori_loop(0, send.shape[0], gather, 0)

    in_arrays = ((k_send, kb), (v_send, vb), (q_send, qb), (g_send, gb))
    job_arrays = ((k_send, jk), (v_send, jv), (q_send, jq), (g_send, jg))
    arrived = {}
    job_arrived = []

    def send_in(g, a):
        src, dst = in_arrays[a]
        for offset in range(1, n):
            target = lax.rem(me + offset, n)
            sends = receives = None
            if a >= 2:
                sends = chip >= first_row(lax.div(target, CORES))
                receives = lax.div(lax.rem(me + n - offset, n), CORES) >= first_row(chip)
            copy = remote(src.at[target * groups + g], dst.at[g, row_of(me)], in_send.at[g, offset - 1, a], in_recv.at[g, offset - 1, a], peer(offset))
            arrived[g, offset, a] = launch(copy, sends, receives)
        arrived[g, 0, a] = local(src.at[me * groups + g], dst.at[g, row_of(me)], in_local.at[g, a])

    def job_head(slot, which_core):
        owner_chip = jnp.where(chip == 0, 1 + slot // groups, chips - 1)
        return (CORES * owner_chip + which_core) * groups + slot % groups

    def job_rows(slot):
        return (slot * (chip + 1) + chip) * blk

    def tokens_at(base, which_core):
        return pl.ds(pl.multiple_of(base + which_core * tokens, tokens), tokens)

    def send_job(a):
        src, dst = job_arrays[a]
        for s in range(slots):
            base = job_rows(s) if a < 2 else s * blk
            place = dst.at[tokens_at(base, core)]
            copy = remote(src.at[job_head(s, 1 - core)], place, ji_send.at[s, a], ji_recv.at[s, a], partner)
            job_arrived.append((landed, launch(copy, s < jobs, s < jobs)))
            job_arrived.append((done, local(src.at[job_head(s, core)], place, ji_local.at[s, a], s < jobs)))

    done(stage_copies[0])
    split_heads(k_stage, k_send)
    done(stage_copies[1])
    split_heads(v_stage, v_send)
    pl.semaphore_wait(barrier, n - 1)
    send_job(0)
    for k in range(CORES):
        for g in range(groups):
            for a in range(2):
                src, dst = job_arrays[a]
                copy = remote(
                    src.at[(CORES * (chips - 1) + k) * groups + g],
                    dst.at[tokens_at(g * 2 * blk, core)],
                    jk_send.at[k, g, a],
                    jk_recv.at[core, g, a],
                    {"cp": CORES + k},
                )
                launch(copy, chip == 0)
    send_in(0, 0)
    done(stage_copies[2])
    split_heads(q_stage, q_send)
    send_job(1)
    send_job(2)
    send_in(0, 1)
    done(stage_copies[3])
    split_heads(g_stage, g_send)
    send_in(0, 2)
    send_job(3)
    send_in(0, 3)
    for g in range(1, groups):
        for a in range(4):
            send_in(g, a)

    key_pos = lax.broadcasted_iota(jnp.int32, (blk, blk), 0)
    query_pos = lax.broadcasted_iota(jnp.int32, (blk, blk), 1)

    def fold(x, op):
        return op(x.reshape(blk // 8, 8, cols), axis=0)

    def prepare(j, key, value):
        rows = block_of(j)
        kt[:, rows] = jnp.transpose(key(j).astype(F32)).astype(BF16)
        vt[:, rows] = jnp.transpose(value(j).astype(F32)).astype(BF16)
        dk_acc[rows, :] = jnp.zeros((blk, dim), F32)
        dv_acc[rows, :] = jnp.zeros((blk, dim), F32)

    def block(i, key, value, query, cotangent, put_lse, put_out, put_dq):
        rows_i = block_of(i)
        for r in range(ratio):
            q_cat[r * blk:(r + 1) * blk, :] = query(r)
            g_cat[r * blk:(r + 1) * blk, :] = cotangent(r)

        def score(j, top):
            s = lax.dot_general(key(j), q_cat[...], NT, preferred_element_type=F32)
            s_scr[block_of(j), :] = s
            return jnp.maximum(top, fold(s, jnp.max))

        top = lax.fori_loop(0, i, score, jnp.full((8, cols), -jnp.inf, F32))
        s = lax.dot_general(key(i), q_cat[...], NT, preferred_element_type=F32)
        keep = jnp.concatenate([key_pos <= query_pos] * ratio, axis=1)
        s = jnp.where(keep, s, -jnp.inf)
        s_scr[rows_i, :] = s
        top = jnp.max(jnp.maximum(top, fold(s, jnp.max)), axis=0, keepdims=True)

        def weigh(j, total):
            rows = block_of(j)
            p = jnp.exp((s_scr[rows, :] - top) * scale)
            s_scr[rows, :] = p
            return total + fold(p, jnp.sum)

        total = lax.fori_loop(0, i + 1, weigh, jnp.zeros((8, cols), F32))
        total = jnp.sum(total, axis=0, keepdims=True)
        inv = 1.0 / total
        lse = top * scale + jnp.log(total)
        for r in range(ratio):
            for t in range(CORES):
                at = r * blk + t * tokens
                put_lse(r, t, lse[:, at:at + tokens])
        t_scr[...] = jnp.zeros((dim, cols), F32)

        def outputs(j, _):
            rows = block_of(j)
            p_low = (s_scr[rows, :] * inv).astype(BF16)
            t_scr[...] += jnp.dot(vt[:, rows], p_low, preferred_element_type=F32)
            dv_acc[rows, :] += jnp.dot(p_low, g_cat[...], preferred_element_type=F32)
            return 0

        lax.fori_loop(0, i + 1, outputs, 0)
        out = jnp.transpose(t_scr[...]).astype(BF16)
        for r in range(ratio):
            put_out(r, out[r * blk:(r + 1) * blk])
        delta = jnp.sum(jnp.transpose(g_cat[...].astype(F32) * out.astype(F32)), axis=0, keepdims=True)
        t_scr[...] = jnp.zeros((dim, cols), F32)

        def gradients(j, _):
            rows = block_of(j)
            dp = lax.dot_general(value(j), g_cat[...], NT, preferred_element_type=F32)
            ds = ((s_scr[rows, :] * inv) * (dp - delta)).astype(BF16)
            t_scr[...] += jnp.dot(kt[:, rows], ds, preferred_element_type=F32)
            dk_acc[rows, :] += jnp.dot(ds, q_cat[...], preferred_element_type=F32)
            return 0

        lax.fori_loop(0, i + 1, gradients, 0)
        dq = jnp.transpose(t_scr[...] * scale).astype(BF16)
        for r in range(ratio):
            put_dq(r, dq[r * blk:(r + 1) * blk])

    for wait, entry in job_arrived:
        wait(entry)
    for j in range(CORES):
        for g in range(groups):
            for a in range(2):
                src, dst = job_arrays[a]
                copy = remote(src.at[0], dst.at[tokens_at(g * 2 * blk, j)], jk_send.at[0, g, a], jk_recv.at[j, g, a], partner)
                landed((copy, chip == 1))

    def job(s, _):
        def key(j):
            return jk[pl.ds(pl.multiple_of((s * (chip + 1) + j) * blk, blk), blk), :]

        def value(j):
            return jv[pl.ds(pl.multiple_of((s * (chip + 1) + j) * blk, blk), blk), :]

        def lanes(r):
            return slice(r * dim, (r + 1) * dim)

        rows = block_of(s)
        group = lax.div(s, groups)
        stat = lax.rem(s, groups) * ratio

        def put_lse(r, t, x):
            jl[group, t, pl.ds(stat + r, 1), :] = x

        def put_out(r, x):
            jq[rows, lanes(r)] = x

        def put_dq(r, x):
            jg[rows, lanes(r)] = x

        def prep(j, _):
            prepare(j, key, value)
            return 0

        lax.fori_loop(0, chip + 1, prep, 0)
        block(chip, key, value, lambda r: jq[rows, lanes(r)], lambda r: jg[rows, lanes(r)], put_lse, put_out, put_dq)
        own = block_of(chip)
        j_own[s, 0] = dk_acc[own, :] * scale
        j_own[s, 1] = dv_acc[own, :]

        @pl.when(chip == 1)
        def _():
            j_part[s, 0] = dk_acc[0:blk, :] * scale
            j_part[s, 1] = dv_acc[0:blk, :]

        return 0

    lax.fori_loop(0, jobs, job, 0)

    closing = []
    for g in range(groups):
        copy = remote(j_part.at[g], j_recv.at[slots + g], j_part_send.at[g], part_recv.at[slots + g], {"cp": core})
        launch(copy, chip == 1)
    for s in range(slots):
        for a, (src, dst) in enumerate(((jq, o_out), (jg, dq_out))):
            place = dst.at[:, column_of(job_head(s, core), wide)]
            copy = remote(src.at[tokens_at(s * blk, 1 - core)], place, jo_send.at[s, a], jo_recv.at[s, a], partner)
            closing.append((landed, launch(copy, s < jobs, s < jobs)))
            closing.append((done, local(src.at[tokens_at(s * blk, core)], place, jo_local.at[s, a], s < jobs)))
    for c in range(chips - 1):
        busy = c * groups < jobs
        owner = CORES * jnp.where(chip == 0, 1 + c, chips - 1) + core
        copy = remote(jl.at[c, 1 - core], lse_out.at[owner], jl_send.at[c], jl_recv.at[c], partner)
        closing.append((landed, launch(copy, busy, busy)))
        closing.append((done, local(jl.at[c, core], lse_out.at[owner], jl_local.at[c], busy)))

    def head_compute(g):
        def key(j):
            return kb[g, block_of(j), :]

        def value(j):
            return vb[g, block_of(j), :]

        def lanes(r):
            return slice(r * dim, (r + 1) * dim)

        def prep(j, _):
            prepare(j, key, value)
            return 0

        lax.fori_loop(0, chips, prep, 0)

        def row(i, _):
            rows = block_of(i)

            def put_lse(r, t, x):
                lseb[i * CORES + t, pl.ds(g * ratio + r, 1), :] = x

            def put_out(r, x):
                ob[g, rows, lanes(r)] = x

            def put_dq(r, x):
                dqb[g, rows, lanes(r)] = x

            block(i, key, value, lambda r: qb[g, rows, lanes(r)], lambda r: gb[g, rows, lanes(r)], put_lse, put_out, put_dq)
            return 0

        lax.fori_loop(first_row(chip), chips, row, 0)

        def finish(j, _):
            rows = block_of(j)
            dkb[g, rows, :] = (dk_acc[rows, :] * scale).astype(BF16)
            dvb[g, rows, :] = dv_acc[rows, :].astype(BF16)
            return 0

        lax.fori_loop(first_row(chip), chips, finish, 0)
        for b in range(JOB_CHIPS):
            @pl.when(b < first_row(chip))
            def _():
                o_part[g, b, 0] = dk_acc[b * blk:(b + 1) * blk, :] * scale
                o_part[g, b, 1] = dv_acc[b * blk:(b + 1) * blk, :]

    out_arrays = ((ob, o_out, wide), (dqb, dq_out, wide), (dkb, dk_out, dim), (dvb, dv_out, dim))
    for g in range(groups):
        for offset in range(n):
            for a in range(4):
                (landed if offset else done)(arrived[g, offset, a])
        head_compute(g)
        for b in range(JOB_CHIPS):
            slot = (chip - 1) * groups + g if b == 0 else g
            sends = b < first_row(chip)
            slot = jnp.where(sends, slot, 0)
            copy = remote(o_part.at[g, b], j_recv.at[slot], o_part_send.at[g, b], part_recv.at[slot], {"cp": CORES * b + core})
            launch(copy, sends)
        for offset in range(1, n):
            target = lax.rem(me + offset, n)
            sends = lax.div(target, CORES) >= first_row(chip)
            receives = chip >= first_row(lax.div(lax.rem(me + n - offset, n), CORES))
            for a, (src, dst, width) in enumerate(out_arrays):
                copy = remote(src.at[g, row_of(target)], dst.at[:, column_of(me * groups + g, width)], out_send.at[g, offset - 1, a], out_recv.at[g, offset - 1, a], peer(offset))
                closing.append((landed, launch(copy, sends, receives)))
        for a, (src, dst, width) in enumerate(out_arrays):
            closing.append((done, local(src.at[g, row_of(me)], dst.at[:, column_of(me * groups + g, width)], out_local.at[g, a])))

    for offset in range(1, n):
        target = lax.rem(me + offset, n)
        sends = lax.div(target, CORES) >= first_row(chip)
        receives = chip >= first_row(lax.div(lax.rem(me + n - offset, n), CORES))
        copy = remote(lseb.at[target], lse_out.at[me], lse_send.at[offset - 1], lse_recv.at[offset - 1], peer(offset))
        closing.append((landed, launch(copy, sends, receives)))
    closing.append((done, local(lseb.at[me], lse_out.at[me], lse_local)))

    for s in range(slots + groups):
        wanted = (chip == 0) | ((chip == 1) & (s < groups)) if s < groups else chip == 0
        copy = remote(j_part.at[0], j_recv.at[s], j_part_send.at[0], part_recv.at[s], partner)
        landed((copy, wanted))

    def total_of(s, _):
        last = jnp.where(chip == 0, s - (chips - 2) * groups, -1)
        rows = pl.ds(pl.multiple_of((s * (chip + 1) + chip) * blk, blk), blk)
        for a, dst in enumerate((jk, jv)):
            j_own[s, a] += j_recv[s, a]

            @pl.when(last >= 0)
            def _():
                j_own[s, a] += j_recv[slots + last, a]

            dst[rows, :] = j_own[s, a].astype(BF16)
        return 0

    lax.fori_loop(0, jobs, total_of, 0)
    for s in range(slots):
        for a, (src, dst) in enumerate(((jk, dk_out), (jv, dv_out))):
            place = dst.at[:, column_of(job_head(s, core), dim)]
            base = job_rows(s)
            copy = remote(src.at[tokens_at(base, 1 - core)], place, fin_send.at[s, a], fin_recv.at[s, a], partner)
            closing.append((landed, launch(copy, s < jobs, s < jobs)))
            closing.append((done, local(src.at[tokens_at(base, core)], place, fin_local.at[s, a], s < jobs)))

    for wait, entry in closing:
        wait(entry)
    for wait, cond in pending:
        if cond is None:
            wait()
        else:
            pl.when(cond)(wait)


def solution(mesh):
    n = mesh.shape["cp"]

    def attention_shard(queries, keys, values, out_grad):
        batch, tokens, heads, dim = queries.shape
        kv_heads = keys.shape[2]
        ratio = heads // kv_heads
        groups = kv_heads // n
        total = n * tokens
        wide = ratio * dim
        blk = CORES * tokens
        slots = (n // CORES - 1) * groups
        stats = -(-groups * ratio // 8) * 8

        def flat(x):
            return x.reshape(tokens, x.shape[2], dim)

        any_space = pl.BlockSpec(memory_space=pl.ANY)
        vmem = pltpu.VMEM
        dma = pltpu.SemaphoreType.DMA
        out, dq, dk, dv, lse = pl.pallas_call(
            functools.partial(attention_kernel, n, groups, ratio, tokens, dim),
            out_shape=(
                jax.ShapeDtypeStruct((tokens, heads * dim), BF16),
                jax.ShapeDtypeStruct((tokens, heads * dim), BF16),
                jax.ShapeDtypeStruct((tokens, kv_heads * dim), BF16),
                jax.ShapeDtypeStruct((tokens, kv_heads * dim), BF16),
                jax.ShapeDtypeStruct((n, stats, tokens), F32),
            ),
            in_specs=[any_space] * 4,
            out_specs=(any_space,) * 5,
            scratch_shapes=[
                vmem((groups, total, wide), BF16),
                vmem((groups, total, dim), BF16),
                vmem((groups, total, dim), BF16),
                vmem((groups, total, wide), BF16),
                vmem((groups, total, wide), BF16),
                vmem((groups, total, wide), BF16),
                vmem((groups, total, dim), BF16),
                vmem((groups, total, dim), BF16),
                vmem((n, stats, tokens), F32),
                vmem((total, ratio * blk), F32),
                vmem((total, dim), F32),
                vmem((total, dim), F32),
                vmem((dim, total), BF16),
                vmem((dim, total), BF16),
                vmem((dim, ratio * blk), F32),
                vmem((ratio * blk, dim), BF16),
                vmem((ratio * blk, dim), BF16),
                vmem((tokens, heads, dim), BF16),
                vmem((tokens, kv_heads, dim), BF16),
                vmem((tokens, kv_heads, dim), BF16),
                vmem((tokens, heads, dim), BF16),
                vmem((kv_heads, tokens, wide), BF16),
                vmem((kv_heads, tokens, dim), BF16),
                vmem((kv_heads, tokens, dim), BF16),
                vmem((kv_heads, tokens, wide), BF16),
                vmem((tokens // 2 * (heads + 8), dim), F32),
                vmem((slots * blk, wide), BF16),
                vmem((slots * blk, dim), BF16),
                vmem((slots * blk, dim), BF16),
                vmem((slots * blk, wide), BF16),
                vmem((n // CORES - 1, CORES, stats, tokens), F32),
                vmem((slots, 2, blk, dim), F32),
                vmem((groups, 2, blk, dim), F32),
                vmem((slots + groups, 2, blk, dim), F32),
                vmem((groups, JOB_CHIPS, 2, blk, dim), F32),
                dma((4,)),
                dma((groups, n - 1, 4)),
                dma((groups, n - 1, 4)),
                dma((groups, n - 1, 4)),
                dma((groups, n - 1, 4)),
                dma((n - 1,)),
                dma((n - 1,)),
                dma((groups, 4)),
                dma((groups, 4)),
                dma,
                dma((slots, 4)),
                dma((slots, 4)),
                dma((slots, 4)),
                dma((CORES, groups, 2)),
                dma((CORES, groups, 2)),
                dma((slots, 2)),
                dma((slots, 2)),
                dma((slots, 2)),
                dma((n // CORES - 1,)),
                dma((n // CORES - 1,)),
                dma((n // CORES - 1,)),
                dma((groups, JOB_CHIPS)),
                dma((groups,)),
                dma((slots + groups,)),
                dma((slots, 2)),
                dma((slots, 2)),
                dma((slots, 2)),
            ],
            compiler_params=pltpu.CompilerParams(collective_id=0, has_side_effects=True, vmem_limit_bytes=62 * 2**20),
            name="heads_attention",
        )(flat(queries), flat(keys), flat(values), flat(out_grad))
        shape = (batch, tokens, heads, dim)
        kv_shape = (batch, tokens, kv_heads, dim)
        row_lse = lse[:, :groups * ratio, :].reshape(batch, heads, tokens)
        return out.reshape(shape), row_lse, dq.reshape(shape), dk.reshape(kv_shape), dv.reshape(kv_shape)

    seq_spec = P("dp", "cp")
    return jax.shard_map(attention_shard, mesh=mesh, in_specs=(seq_spec,) * 4, out_specs=(seq_spec, P("dp", None, "cp"), seq_spec, seq_spec, seq_spec), check_vma=False)
```

time: 164 us -> 152 us (0.927)
  local copies, waits for them, and re-layouts: 18 us -> 8.35 us
  Pallas kernels: 145 us -> 142 us
    reshape x2 -> x0, local copies, waits for them, and re-layouts: 9.64 us -> none  [flat(): return x.reshape(tokens, x.shape[2] * dim)]
    pallas_call x1, Pallas kernels: 145 us -> 142 us  [attention_shard(): pl.pallas_call(functools.partial(attention_kernel, n, groups, ratio, toke...]
    unnamed x16 -> x12, local copies, waits for them, and re-layouts: 7.72 us -> 7.72 us
where the time goes in v4:
time: 152 us; the launch traced here: 151 us
  Pallas kernels  142 us (93%)
  local copies, waits for them, and re-layouts  8.35 us (5%)
    pallas_call x1, Pallas kernels, attention_shard(): pl.pallas_call(functools.partial(attention_kernel, n, groups, ratio, toke...  142 us
    unnamed x12, local copies, waits for them, and re-layouts  7.72 us

profile of v4, /device:TPU:81, one launch (start us, length us, event | category | flops | bytes accessed | tf_op | source)
XLA Modules:
  0.0 151.5 jit_solution(12842855945420289087)
XLA Ops:
  0.6 142.5 %heads_attention.1 = (bf16[256,4096]{1,0:T(8,128)(2,1)}, bf16[256,4096]{1,0:T(8,128)(2,1)}, bf16[256,2048]{1,0:T(8,128)(2,1)}, bf16[256,2048]{1,0:T(8,128)(2,1)}, f32[8,8,256]{2,1,0:T(8,128)}) custom-call(bf16[256,32,128]{2,1,0:T(8,128)(2,1)} %bitcast.16, bf16[256,16,128]{2,1,0:T(8,128)(2,1)} %bitcast.26, bf16[256,16,128]{2,1,0:T(8,128)(2,1)} %bitcast.27, ...), custom_call_target="tpu_custom_call" | custom-call | tf_op jit(solution)/shard_map/heads_attention/pallas_call | solution.py:455
  143.1 0.0 copy-start.3
  143.1 0.0 copy-start.2
  143.1 3.5 %copy.9 = bf16[32,8,32,128]{3,2,1,0:T(8,128)(2,1)} copy(bf16[32,8,32,128]{3,1,2,0:T(8,128)(2,1)} %bitcast.21) | data formatting | bytes 4194304
  146.6 0.0 copy-start.1
  146.6 0.0 copy-done.3
  146.6 0.6 reshape.42
  147.2 0.0 copy-done.2
  147.3 0.0 copy-start
  147.3 1.2 copy.11
  148.5 0.0 copy-done.1
  148.5 1.2 copy.12
  149.7 0.0 copy-done
  149.7 1.8 %copy.10 = bf16[32,8,32,128]{3,2,1,0:T(8,128)(2,1)} copy(bf16[32,8,32,128]{3,1,2,0:T(8,128)(2,1)S(1)} %bitcast.19) | data formatting | bytes 4194304
  (1 shorter events, 0.0 us)
Async XLA Ops:
  143.1 3.5 %copy-start.3 = (f32[8,8,256]{2,1,0:T(8,128)S(1)}, f32[8,8,256]{2,1,0:T(8,128)}, u32[]{:S(2)}) copy-start(f32[8,8,256]{2,1,0:T(8,128)} %get-tuple-element.11) | copy-start | bytes 196612
  143.1 4.1 %copy-start.2 = (bf16[256,2048]{1,0:T(8,128)(2,1)S(1)}, bf16[256,2048]{1,0:T(8,128)(2,1)}, u32[]{:S(2)}) copy-start(bf16[256,2048]{1,0:T(8,128)(2,1)} %get-tuple-element.13) | copy-start | bytes 3145732
  146.6 1.9 %copy-start.1 = (bf16[256,2048]{1,0:T(8,128)(2,1)S(1)}, bf16[256,2048]{1,0:T(8,128)(2,1)}, u32[]{:S(2)}) copy-start(bf16[256,2048]{1,0:T(8,128)(2,1)} %get-tuple-element.14) | copy-start | bytes 3145732
  147.3 2.4 %copy-start = (bf16[256,4096]{1,0:T(8,128)(2,1)S(1)}, bf16[256,4096]{1,0:T(8,128)(2,1)}, u32[]{:S(2)}) copy-start(bf16[256,4096]{1,0:T(8,128)(2,1)} %get-tuple-element.12) | copy-start | bytes 6291460

commit v5 on v4

--- a/solution.py
+++ b/solution.py
@@ -55,7 +55,7 @@
             copy.start()
         else:
             pl.when(sends)(copy.start)
-        pending.append((copy.wait_send, sends))
+        pending.append((send_done, (copy, sends)))
         return (copy, receives)
 
     def landed(entry):
@@ -64,6 +64,13 @@
             copy.wait_recv()
         else:
             pl.when(receives)(copy.wait_recv)
+
+    def send_done(entry):
+        copy, sends = entry
+        if sends is None:
+            copy.wait_send()
+        else:
+            pl.when(sends)(copy.wait_send)
 
     def local(src, dst, sem, cond=None):
         copy = pltpu.make_async_copy(src, dst, sem)
@@ -148,8 +155,9 @@
     done(stage_copies[0])
     split_heads(k_stage, k_send)
     done(stage_copies[1])
+    pl.semaphore_wait(barrier, n - 1)
+    send_in(0, 0)
     split_heads(v_stage, v_send)
-    pl.semaphore_wait(barrier, n - 1)
     send_job(0)
     for k in range(CORES):
         for g in range(groups):
@@ -163,7 +171,6 @@
                     {"cp": CORES + k},
                 )
                 launch(copy, chip == 0)
-    send_in(0, 0)
     done(stage_copies[2])
     split_heads(q_stage, q_send)
     send_job(1)
@@ -320,6 +327,18 @@
         closing.append((landed, launch(copy, busy, busy)))
         closing.append((done, local(jl.at[c, core], lse_out.at[owner], jl_local.at[c], busy)))
 
+    out_arrays = ((ob, o_out, wide), (dqb, dq_out, wide), (dkb, dk_out, dim), (dvb, dv_out, dim))
+
+    def out_copy(g, offset, a):
+        src, dst, width = out_arrays[a]
+        target = lax.rem(me + offset, n)
+        at = lax.rem(offset + n - 1, n)
+        return remote(src.at[g, row_of(target)], dst.at[:, column_of(me * groups + g, width)], out_send.at[g, at, a], out_recv.at[g, at, a], peer(offset))
+
+    def own_copy(g, a):
+        src, dst, width = out_arrays[a]
+        return pltpu.make_async_copy(src.at[g, row_of(me)], dst.at[:, column_of(me * groups + g, width)], out_local.at[g, a])
+
     def head_compute(g):
         def key(j):
             return kb[g, block_of(j), :]
@@ -336,7 +355,8 @@
 
         lax.fori_loop(0, chips, prep, 0)
 
-        def row(i, _):
+        def row(step, _):
+            i = chips - 1 - step
             rows = block_of(i)
 
             def put_lse(r, t, x):
@@ -349,25 +369,28 @@
                 dqb[g, rows, lanes(r)] = x
 
             block(i, key, value, lambda r: qb[g, rows, lanes(r)], lambda r: gb[g, rows, lanes(r)], put_lse, put_out, put_dq)
-            return 0
-
-        lax.fori_loop(first_row(chip), chips, row, 0)
-
-        def finish(j, _):
-            rows = block_of(j)
             dkb[g, rows, :] = (dk_acc[rows, :] * scale).astype(BF16)
             dvb[g, rows, :] = dv_acc[rows, :].astype(BF16)
+            early = True if g < groups - 1 else (chip == 0) | ((i < chips - 1) != (chip == chips - 1))
+            for t in range(CORES):
+                target = i * CORES + t
+                for a in range(4):
+                    pl.when((target != me) & early)(out_copy(g, lax.rem(target + n - me, n), a).start)
+                    pl.when(target == me)(own_copy(g, a).start)
             return 0
 
-        lax.fori_loop(first_row(chip), chips, finish, 0)
+        lax.fori_loop(0, chips - first_row(chip), row, 0)
         for b in range(JOB_CHIPS):
             @pl.when(b < first_row(chip))
             def _():
                 o_part[g, b, 0] = dk_acc[b * blk:(b + 1) * blk, :] * scale
                 o_part[g, b, 1] = dv_acc[b * blk:(b + 1) * blk, :]
 
-    out_arrays = ((ob, o_out, wide), (dqb, dq_out, wide), (dkb, dk_out, dim), (dvb, dv_out, dim))
+    early_waits = []
+    late_waits = []
     for g in range(groups):
+        last = g == groups - 1
+        waits = late_waits if last else early_waits
         for offset in range(n):
             for a in range(4):
                 (landed if offset else done)(arrived[g, offset, a])
@@ -380,56 +403,64 @@
             launch(copy, sends)
         for offset in range(1, n):
             target = lax.rem(me + offset, n)
-            sends = lax.div(target, CORES) >= first_row(chip)
+            target_chip = lax.div(target, CORES)
+            sends = target_chip >= first_row(chip)
             receives = chip >= first_row(lax.div(lax.rem(me + n - offset, n), CORES))
-            for a, (src, dst, width) in enumerate(out_arrays):
-                copy = remote(src.at[g, row_of(target)], dst.at[:, column_of(me * groups + g, width)], out_send.at[g, offset - 1, a], out_recv.at[g, offset - 1, a], peer(offset))
-                closing.append((landed, launch(copy, sends, receives)))
-        for a, (src, dst, width) in enumerate(out_arrays):
-            closing.append((done, local(src.at[g, row_of(me)], dst.at[:, column_of(me * groups + g, width)], out_local.at[g, a])))
+            for a in range(4):
+                copy = out_copy(g, offset, a)
+                if last:
+                    pl.when(sends & ((target_chip >= chips - 1) != (chip == chips - 1)) & (chip > 0))(copy.start)
+                waits.append((send_done, (copy, sends)))
+                waits.append((landed, (copy, receives)))
+        for a in range(4):
+            waits.append((done, (own_copy(g, a), None)))
 
     for offset in range(1, n):
         target = lax.rem(me + offset, n)
         sends = lax.div(target, CORES) >= first_row(chip)
         receives = chip >= first_row(lax.div(lax.rem(me + n - offset, n), CORES))
         copy = remote(lseb.at[target], lse_out.at[me], lse_send.at[offset - 1], lse_recv.at[offset - 1], peer(offset))
-        closing.append((landed, launch(copy, sends, receives)))
-    closing.append((done, local(lseb.at[me], lse_out.at[me], lse_local)))
-
-    for s in range(slots + groups):
-        wanted = (chip == 0) | ((chip == 1) & (s < groups)) if s < groups else chip == 0
-        copy = remote(j_part.at[0], j_recv.at[s], j_part_send.at[0], part_recv.at[s], partner)
-        landed((copy, wanted))
-
-    def total_of(s, _):
-        last = jnp.where(chip == 0, s - (chips - 2) * groups, -1)
-        rows = pl.ds(pl.multiple_of((s * (chip + 1) + chip) * blk, blk), blk)
+        pl.when(sends)(copy.start)
+        late_waits.append((send_done, (copy, sends)))
+        late_waits.append((landed, (copy, receives)))
+    late_waits.append((done, local(lseb.at[me], lse_out.at[me], lse_local)))
+
+    for wait, entry in closing + pending + early_waits:
+        wait(entry)
+
+    def total_of(s):
+        tail = s - (chips - 2) * groups
+        rows = pl.ds(pl.multiple_of(job_rows(s), blk), blk)
         for a, dst in enumerate((jk, jv)):
-            j_own[s, a] += j_recv[s, a]
-
-            @pl.when(last >= 0)
-            def _():
-                j_own[s, a] += j_recv[slots + last, a]
-
-            dst[rows, :] = j_own[s, a].astype(BF16)
-        return 0
-
-    lax.fori_loop(0, jobs, total_of, 0)
-    for s in range(slots):
-        for a, (src, dst) in enumerate(((jk, dk_out), (jv, dv_out))):
-            place = dst.at[:, column_of(job_head(s, core), dim)]
-            base = job_rows(s)
-            copy = remote(src.at[tokens_at(base, 1 - core)], place, fin_send.at[s, a], fin_recv.at[s, a], partner)
-            closing.append((landed, launch(copy, s < jobs, s < jobs)))
-            closing.append((done, local(src.at[tokens_at(base, core)], place, fin_local.at[s, a], s < jobs)))
-
-    for wait, entry in closing:
+            if tail >= 0:
+                @pl.when(chip == 0)
+                def _():
+                    j_own[s, a] += j_recv[slots + tail, a]
+
+            dst[rows, :] = (j_own[s, a] + j_recv[s, a]).astype(BF16)
+
+    final = []
+    for g in range(groups):
+        if g == groups - 1:
+            for wait, entry in late_waits:
+                wait(entry)
+        for s in range(g, slots + groups, groups):
+            wanted = chip <= 1 if s < groups else chip == 0
+            copy = remote(j_part.at[0], j_recv.at[s], j_part_send.at[0], part_recv.at[s], partner)
+            landed((copy, wanted))
+        for s in range(g, slots, groups):
+            pl.when(s < jobs)(functools.partial(total_of, s))
+        for s in range(g, slots, groups):
+            for a, (src, dst) in enumerate(((jk, dk_out), (jv, dv_out))):
+                place = dst.at[:, column_of(job_head(s, core), dim)]
+                base = job_rows(s)
+                copy = remote(src.at[tokens_at(base, 1 - core)], place, fin_send.at[s, a], fin_recv.at[s, a], partner)
+                pl.when(s < jobs)(copy.start)
+                final.append((send_done, (copy, s < jobs)))
+                final.append((landed, (copy, s < jobs)))
+                final.append((done, local(src.at[tokens_at(base, core)], place, fin_local.at[s, a], s < jobs)))
+    for wait, entry in final:
         wait(entry)
-    for wait, cond in pending:
-        if cond is None:
-            wait()
-        else:
-            pl.when(cond)(wait)
 
 
 def solution(mesh):
@@ -502,8 +533,8 @@
                 dma((4,)),
                 dma((groups, n - 1, 4)),
                 dma((groups, n - 1, 4)),
-                dma((groups, n - 1, 4)),
-                dma((groups, n - 1, 4)),
+                dma((groups, n, 4)),
+                dma((groups, n, 4)),
                 dma((n - 1,)),
                 dma((n - 1,)),
                 dma((groups, 4)),

time: 152 us -> 144 us (0.947); the launches traced: 151 us -> 141 us
  Pallas kernels: 142 us -> 132 us
    pallas_call x1, Pallas kernels: 142 us -> 132 us  [attention_shard(): pl.pallas_call(functools.partial(attention_kernel, n, groups, ratio, toke...]
where the time goes in v5:
time: 144 us; the launch traced here: 141 us
  Pallas kernels  132 us (92%)
  local copies, waits for them, and re-layouts  8.35 us (6%)
    pallas_call x1, Pallas kernels, attention_shard(): pl.pallas_call(functools.partial(attention_kernel, n, groups, ratio, toke...  132 us
    unnamed x12, local copies, waits for them, and re-layouts  7.72 us

profile of v5, /device:TPU:81, one launch (start us, length us, event | category | flops | bytes accessed | tf_op | source)
XLA Modules:
  0.0 141.1 jit_solution(2942669820922623205)
XLA Ops:
  0.6 132.1 %heads_attention.1 = (bf16[256,4096]{1,0:T(8,128)(2,1)}, bf16[256,4096]{1,0:T(8,128)(2,1)}, bf16[256,2048]{1,0:T(8,128)(2,1)}, bf16[256,2048]{1,0:T(8,128)(2,1)}, f32[8,8,256]{2,1,0:T(8,128)}) custom-call(bf16[256,32,128]{2,1,0:T(8,128)(2,1)} %bitcast.16, bf16[256,16,128]{2,1,0:T(8,128)(2,1)} %bitcast.26, bf16[256,16,128]{2,1,0:T(8,128)(2,1)} %bitcast.27, ...), custom_call_target="tpu_custom_call" | custom-call | tf_op jit(solution)/shard_map/heads_attention/pallas_call | solution.py:486
  132.7 0.0 copy-start.3
  132.7 0.0 copy-start.2
  132.7 3.5 %copy.9 = bf16[32,8,32,128]{3,2,1,0:T(8,128)(2,1)} copy(bf16[32,8,32,128]{3,1,2,0:T(8,128)(2,1)} %bitcast.21) | data formatting | bytes 4194304
  136.2 0.0 copy-start.1
  136.2 0.0 copy-done.3
  136.2 0.6 reshape.42
  136.8 0.0 copy-done.2
  136.8 0.0 copy-start
  136.8 1.2 copy.11
  138.1 0.0 copy-done.1
  138.1 1.2 copy.12
  139.3 0.0 copy-done
  139.3 1.8 %copy.10 = bf16[32,8,32,128]{3,2,1,0:T(8,128)(2,1)} copy(bf16[32,8,32,128]{3,1,2,0:T(8,128)(2,1)S(1)} %bitcast.19) | data formatting | bytes 4194304
  (1 shorter events, 0.0 us)
Async XLA Ops:
  132.7 3.5 %copy-start.3 = (f32[8,8,256]{2,1,0:T(8,128)S(1)}, f32[8,8,256]{2,1,0:T(8,128)}, u32[]{:S(2)}) copy-start(f32[8,8,256]{2,1,0:T(8,128)} %get-tuple-element.11) | copy-start | bytes 196612
  132.7 4.1 %copy-start.2 = (bf16[256,2048]{1,0:T(8,128)(2,1)S(1)}, bf16[256,2048]{1,0:T(8,128)(2,1)}, u32[]{:S(2)}) copy-start(bf16[256,2048]{1,0:T(8,128)(2,1)} %get-tuple-element.13) | copy-start | bytes 3145732
  136.2 1.9 %copy-start.1 = (bf16[256,2048]{1,0:T(8,128)(2,1)S(1)}, bf16[256,2048]{1,0:T(8,128)(2,1)}, u32[]{:S(2)}) copy-start(bf16[256,2048]{1,0:T(8,128)(2,1)} %get-tuple-element.14) | copy-start | bytes 3145732
  136.8 2.4 %copy-start = (bf16[256,4096]{1,0:T(8,128)(2,1)S(1)}, bf16[256,4096]{1,0:T(8,128)(2,1)}, u32[]{:S(2)}) copy-start(bf16[256,4096]{1,0:T(8,128)(2,1)} %get-tuple-element.12) | copy-start | bytes 6291460

commit v6 on v5

--- a/solution.py
+++ b/solution.py
@@ -15,7 +15,7 @@
 JOB_CHIPS = 2
 
 
-def attention_kernel(n, groups, ratio, tokens, dim, q_in, k_in, v_in, g_in, o_out, dq_out, dk_out, dv_out, lse_out, qb, kb, vb, gb, ob, dqb, dkb, dvb, lseb, s_scr, dk_acc, dv_acc, kt, vt, t_scr, q_cat, g_cat, q_stage, k_stage, v_stage, g_stage, q_send, k_send, v_send, g_send, f_scr, jq, jk, jv, jg, jl, j_own, j_part, j_recv, o_part, stage_sem, in_send, in_recv, out_send, out_recv, lse_send, lse_recv, in_local, out_local, lse_local, ji_send, ji_recv, ji_local, jk_send, jk_recv, jo_send, jo_recv, jo_local, jl_send, jl_recv, jl_local, o_part_send, j_part_send, part_recv, fin_send, fin_recv, fin_local):
+def attention_kernel(n, groups, ratio, tokens, dim, q_in, k_in, v_in, g_in, o_out, dq_out, dk_out, dv_out, lse_out, qb, kb, vb, gb, ob, dqb, dkb, dvb, lseb, s_scr, dk_acc, dv_acc, kt, vt, t_scr, q_cat, g_cat, q_stage, k_stage, v_stage, q_send, k_send, v_send, g_send, f_scr, jq, jk, jv, jg, jl, j_own, j_part, j_recv, o_part, stage_sem, in_send, in_recv, out_send, out_recv, lse_send, lse_recv, in_local, out_local, lse_local, ji_send, ji_recv, ji_local, jk_send, jk_recv, jo_send, jo_recv, jo_local, jl_send, jl_recv, jl_local, o_part_send, j_part_send, part_recv, fin_send, fin_recv, fin_local):
     me = lax.axis_index("cp")
     chip = lax.div(me, CORES)
     core = lax.rem(me, CORES)
@@ -87,7 +87,7 @@
         else:
             pl.when(cond)(copy.wait)
 
-    stage_copies = [local(src, dst, stage_sem.at[a]) for a, (src, dst) in enumerate(((k_in, k_stage), (v_in, v_stage), (q_in, q_stage), (g_in, g_stage)))]
+    stage_copies = [local(src, dst, stage_sem.at[a]) for a, (src, dst) in enumerate(((k_in, k_stage), (v_in, v_stage), (q_in, q_stage)))]
 
     barrier = pltpu.get_barrier_semaphore()
     for offset in range(1, n):
@@ -173,11 +173,12 @@
                 launch(copy, chip == 0)
     done(stage_copies[2])
     split_heads(q_stage, q_send)
+    cotangents = local(g_in, q_stage, stage_sem.at[3])
     send_job(1)
     send_job(2)
     send_in(0, 1)
-    done(stage_copies[3])
-    split_heads(g_stage, g_send)
+    done(cotangents)
+    split_heads(q_stage, g_send)
     send_in(0, 2)
     send_job(3)
     send_in(0, 3)
@@ -441,9 +442,6 @@
 
     final = []
     for g in range(groups):
-        if g == groups - 1:
-            for wait, entry in late_waits:
-                wait(entry)
         for s in range(g, slots + groups, groups):
             wanted = chip <= 1 if s < groups else chip == 0
             copy = remote(j_part.at[0], j_recv.at[s], j_part_send.at[0], part_recv.at[s], partner)
@@ -459,7 +457,7 @@
                 final.append((send_done, (copy, s < jobs)))
                 final.append((landed, (copy, s < jobs)))
                 final.append((done, local(src.at[tokens_at(base, core)], place, fin_local.at[s, a], s < jobs)))
-    for wait, entry in final:
+    for wait, entry in late_waits + final:
         wait(entry)
 
 
@@ -486,14 +484,14 @@
         out, dq, dk, dv, lse = pl.pallas_call(
             functools.partial(attention_kernel, n, groups, ratio, tokens, dim),
             out_shape=(
-                jax.ShapeDtypeStruct((tokens, heads * dim), BF16),
-                jax.ShapeDtypeStruct((tokens, heads * dim), BF16),
-                jax.ShapeDtypeStruct((tokens, kv_heads * dim), BF16),
-                jax.ShapeDtypeStruct((tokens, kv_heads * dim), BF16),
-                jax.ShapeDtypeStruct((n, stats, tokens), F32),
+                pltpu.VMEM((tokens, heads * dim), BF16),
+                pltpu.VMEM((tokens, heads * dim), BF16),
+                pltpu.VMEM((tokens, kv_heads * dim), BF16),
+                pltpu.VMEM((tokens, kv_heads * dim), BF16),
+                pltpu.VMEM((n, stats, tokens), F32),
             ),
             in_specs=[any_space] * 4,
-            out_specs=(any_space,) * 5,
+            out_specs=(pl.BlockSpec(memory_space=pltpu.VMEM),) * 5,
             scratch_shapes=[
                 vmem((groups, total, wide), BF16),
                 vmem((groups, total, dim), BF16),
@@ -515,7 +513,6 @@
                 vmem((tokens, heads, dim), BF16),
                 vmem((tokens, kv_heads, dim), BF16),
                 vmem((tokens, kv_heads, dim), BF16),
-                vmem((tokens, heads, dim), BF16),
                 vmem((kv_heads, tokens, wide), BF16),
                 vmem((kv_heads, tokens, dim), BF16),
                 vmem((kv_heads, tokens, dim), BF16),
@@ -558,7 +555,7 @@
                 dma((slots, 2)),
                 dma((slots, 2)),
             ],
-            compiler_params=pltpu.CompilerParams(collective_id=0, has_side_effects=True, vmem_limit_bytes=62 * 2**20),
+            compiler_params=pltpu.CompilerParams(collective_id=0, has_side_effects=True, vmem_limit_bytes=57 * 2**20),
             name="heads_attention",
         )(flat(queries), flat(keys), flat(values), flat(out_grad))
         shape = (batch, tokens, heads, dim)

time: 144 us -> 141 us (0.979)
  the two profiles are of different devices: /device:TPU:81 before, /device:TPU:91 now
where the time goes in v6:
time: 141 us
  Pallas kernels  134 us (95%)
  local copies, waits for them, and re-layouts  6.86 us (5%)
    pallas_call x1, Pallas kernels, attention_shard(): pl.pallas_call(functools.partial(attention_kernel, n, groups, ratio, toke...  134 us
    unnamed x8, local copies, waits for them, and re-layouts  6.23 us

profile of v6, /device:TPU:91, one launch (start us, length us, event | category | flops | bytes accessed | tf_op | source)
XLA Modules:
  0.0 141.0 jit_solution(2317487452445662680)
XLA Ops:
  0.6 133.5 %heads_attention.1 = (bf16[256,4096]{1,0:T(8,128)(2,1)S(1)}, bf16[256,4096]{1,0:T(8,128)(2,1)S(1)}, bf16[256,2048]{1,0:T(8,128)(2,1)S(1)}, bf16[256,2048]{1,0:T(8,128)(2,1)S(1)}, f32[8,8,256]{2,1,0:T(8,128)S(1)}) custom-call(bf16[256,32,128]{2,1,0:T(8,128)(2,1)} %bitcast.20, bf16[256,16,128]{2,1,0:T(8,128)(2,1)} %bitcast.26, bf16[256,16,128]{2,1,0:T(8,128)(2,1)} %bitcast.27, ...), custom_call_target="tpu_custom_call" | custom-call | tf_op jit(solution)/shard_map/heads_attention/pallas_call | solution.py:484
  134.2 0.0 copy-start
  134.2 2.0 %copy.9 = bf16[32,8,32,128]{3,2,1,0:T(8,128)(2,1)} copy(bf16[32,8,32,128]{3,1,2,0:T(8,128)(2,1)S(1)} %bitcast.17) | data formatting | bytes 4194304
  136.2 0.0 copy-done
  136.2 0.6 reshape.42
  136.8 0.0 copy-start.1
  136.8 1.2 copy.11
  138.0 1.2 copy.12
  139.2 0.0 copy-done.1
  139.2 1.8 %copy.10 = bf16[32,8,32,128]{3,2,1,0:T(8,128)(2,1)} copy(bf16[32,8,32,128]{3,1,2,0:T(8,128)(2,1)S(1)} %bitcast.16) | data formatting | bytes 4194304
  (1 shorter events, 0.0 us)
Async XLA Ops:
  134.2 2.0 %copy-start = (bf16[256,4096]{1,0:T(8,128)(2,1)}, bf16[256,4096]{1,0:T(8,128)(2,1)S(1)}, u32[]{:S(2)}) copy-start(bf16[256,4096]{1,0:T(8,128)(2,1)S(1)} %get-tuple-element.12) | copy-start | bytes 6291460
  136.8 2.4 %copy-start.1 = (bf16[256,4096]{1,0:T(8,128)(2,1)S(1)}, bf16[256,4096]{1,0:T(8,128)(2,1)}, u32[]{:S(2)}) copy-start(bf16[256,4096]{1,0:T(8,128)(2,1)} %copy-done) | copy-start | bytes 6291460
